TPU v7x, 32 devices: a whole 2x2x4 slice. The times are simulated.
32 devices in a mesh: dp: 16 (over z, y, x), tensor: 2 (over core).
Axes of the slice: x: 2, y: 2, z: 4, core: 2. Of those that a mesh axis runs over, the one named last changes fastest.
Arguments:
- tokens: bfloat16 [16384, 768], P(('dp', 'tensor')), may hold values from -6 to 6
- cotangent: bfloat16 [16384, 768], P(('dp', 'tensor')), may hold values from -6 to 6
- prefix: int32 [16], P('dp'), may hold values from 102 to 512, as said below
- routes: int32 [16384, 1], P('dp'), may hold values from 0 to 1; in each aligned block of 1024 rows (0 to 1023, 1024 to 2047, ...) at most 640 rows name the same one
- norm1_gain: float32 [768], P(('dp', 'tensor')), may hold values from 0.5 to 1.5
- norm1_bias: float32 [768], P(('dp', 'tensor')), may hold values from -0.625 to 0.625
- w_query: bfloat16 [768, 768], P('dp', 'tensor'), may hold values from -0.4375 to 0.4375
- w_key: bfloat16 [768, 768], P('dp', 'tensor'), may hold values from -0.21875 to 0.21875
- w_value: bfloat16 [768, 768], P('dp', 'tensor'), may hold values from -0.21875 to 0.21875
- w_out: bfloat16 [768, 768], P('tensor', 'dp'), may hold values from -1.75 to 1.75
- norm2_gain: float32 [768], P(('dp', 'tensor')), may hold values from 0.5 to 1.5
- norm2_bias: float32 [768], P(('dp', 'tensor')), may hold values from -0.625 to 0.625
- centroids: float32 [2, 768], P(None, ('dp', 'tensor')), may hold values from -0.1875 to 0.1875
- expert_in: bfloat16 [2, 768, 3072], P(None, 'dp', 'tensor'), may hold values from -0.21875 to 0.21875
- expert_out: bfloat16 [2, 3072, 768], P(None, 'tensor', 'dp'), may hold values from -0.4375 to 0.4375
Outputs:
- block_out: bfloat16 [16384, 768], P(('dp', 'tensor'))
- grad_tokens: bfloat16 [16384, 768], P(('dp', 'tensor'))
- grad_norm1_gain: float32 [768], P(('dp', 'tensor'))
- grad_norm1_bias: float32 [768], P(('dp', 'tensor'))
- grad_w_query: float32 [768, 768], P('dp', 'tensor')
- grad_w_key: float32 [768, 768], P('dp', 'tensor')
- grad_w_value: float32 [768, 768], P('dp', 'tensor')
- grad_w_out: float32 [768, 768], P('tensor', 'dp')
- grad_norm2_gain: float32 [768], P(('dp', 'tensor'))
- grad_norm2_bias: float32 [768], P(('dp', 'tensor'))
- grad_centroids: float32 [2, 768], P(None, ('dp', 'tensor'))
- grad_expert_in: float32 [2, 768, 3072], P(None, 'dp', 'tensor')
- grad_expert_out: float32 [2, 3072, 768], P(None, 'tensor', 'dp')
Inputs may be any that keep to these rules, and one draw needn't show every extreme that they name: Each sequence's first prefix tokens see one another; some sequence's prefix is exactly half of 1024. `routes`: in each aligned block of 1024 rows (the tokens of one index of dp) no expert is named by more than 640 rows; some block names an expert exactly 640 times.
All inputs are finite; a program needn't handle non-finite values.
Results may differ from a plain program's by a relative error of at most 0.02.
Values may be sent and summed in bfloat16 or wider, within the bound.
A program may use at most 192 MiB of HBM per device.

v0:
```python
import jax
import jax.numpy as jnp
from jax import lax
from jax.experimental import pallas as pl
from jax.experimental.pallas import tpu as pltpu
from jax.sharding import PartitionSpec as P


HEADS = 12
CAP = 640
EPS = 1e-05
NEGATIVE = -1e30
BF = jnp.bfloat16
F32 = jnp.float32
MESH = pl.DeviceIdType.MESH


def factors_of(count):
    rest, sizes = count // 2, []
    while rest % 4 == 0:
        sizes.append(4)
        rest //= 4
    while rest % 2 == 0 and rest > 1:
        sizes.append(2)
        rest //= 2
    return sizes + ([2] if count > 1 else [])


class Ring:
    def __init__(self, count):
        self.count = count
        self.sizes = factors_of(count)
        self.strides = []
        stride = count
        for size in self.sizes:
            stride //= size
            self.strides.append(stride)
        self.square = len(self.sizes) >= 2 and self.sizes[-1] == 2 and self.sizes[-2] == 2

    def order(self, size):
        return [0, 1, 3, 2] if size == 4 else list(range(size))

    def shift(self, stage, step):
        size, stride = self.sizes[stage], self.strides[stage]
        order = self.order(size)
        pairs = []
        for source in range(self.count):
            digit = source // stride % size
            target = order[(order.index(digit) + step) % size]
            pairs.append((source, source + (target - digit) * stride))
        return pairs

    def move(self, value, stage, step):
        return lax.ppermute(value, "dp", self.shift(stage, step))

    def lead(self, block):
        for stage in range(len(self.sizes) - (2 if self.square else 0)):
            parts = [block] + [self.move(block, stage, s) for s in range(1, self.sizes[stage])]
            block = jnp.concatenate(parts, axis=0)
        return block

    def cross(self, block):
        if not self.square:
            return ()
        y, x = len(self.sizes) - 2, len(self.sizes) - 1
        return self.move(block, x, 1), self.move(block, y, 1)

    def close(self, block, crossed):
        if not self.square:
            return block
        y, x = len(self.sizes) - 2, len(self.sizes) - 1
        half = block.shape[0] // 2
        from_x, from_y = crossed
        low, high = self.move(from_y[:half], x, 1), self.move(from_x[half:], y, 1)
        return jnp.concatenate([block, from_y, from_x, low, high], axis=0)

    def gather(self, block):
        block = self.lead(block)
        return self.close(block, self.cross(block))

    def far(self, total, kind):
        if not self.square:
            return ()
        y, x = len(self.sizes) - 2, len(self.sizes) - 1
        quarter = total.shape[0] // 4
        half = quarter // 2
        far = total[3 * quarter :]
        return self.move(far[:half].astype(kind), x, 1), self.move(far[half:].astype(kind), y, 1)

    def near(self, total, via, kind):
        if not self.square:
            return ()
        y, x = len(self.sizes) - 2, len(self.sizes) - 1
        quarter = total.shape[0] // 4
        half = quarter // 2
        via_x, via_y = via
        to_y, to_x = total[quarter : 2 * quarter], total[2 * quarter : 3 * quarter]
        to_y = jnp.concatenate([(to_y[:half].astype(F32) + via_x).astype(kind), to_y[half:].astype(kind)], axis=0)
        to_x = jnp.concatenate([to_x[:half].astype(kind), (to_x[half:].astype(F32) + via_y).astype(kind)], axis=0)
        return self.move(to_x, x, 1), self.move(to_y, y, 1)

    def last(self, total, crossed, kind):
        stages = len(self.sizes)
        if self.square:
            own = total[: total.shape[0] // 4].astype(F32)
            total = own + crossed[0].astype(F32) + crossed[1].astype(F32)
            stages -= 2
        for stage in reversed(range(stages)):
            size = self.sizes[stage]
            piece = total.shape[0] // size
            parts = [total[i * piece : (i + 1) * piece] for i in range(size)]
            total = parts[0].astype(F32)
            for step in range(1, size):
                total = total + self.move(parts[step].astype(kind), stage, size - step).astype(F32)
        return total

    def scatter(self, total, kind):
        return self.last(total, self.near(total, self.far(total, kind), kind), kind)

    def width_order(self, width):
        me = lax.axis_index("dp")
        rows = width // self.count
        column = jnp.arange(width, dtype=jnp.int32)
        inner, block = column % rows, column // rows
        found = jnp.zeros_like(column)
        for size, stride in zip(self.sizes, self.strides):
            step, block = block % size, block // size
            digit = me // stride % size
            if size == 4:
                place = jnp.bitwise_xor(digit, digit // 2)
                back = (place - step + size) % size
                source = jnp.bitwise_xor(back, back // 2)
            else:
                source = (digit - step + size) % size
            found = found + source * stride
        return found * rows + inner


def ring_place(digit):
    return digit + (digit // 2) * (1 - 2 * (digit % 2))


def partners_of(me):
    digit = me // 4
    place = ring_place(digit)
    along = [me + (ring_place((place + step) % 4) - digit) * 4 for step in range(1, 4)]
    return along, me + 1 - 2 * (me % 2), me + 2 - 4 * ((me // 2) % 2)


def greet(along, x_way, y_way, other):
    barrier = pltpu.get_barrier_semaphore()
    for device in along + [x_way, y_way]:
        pl.semaphore_signal(barrier, inc=1, device_id={"dp": device}, device_id_type=MESH)
    pl.semaphore_signal(barrier, inc=1, device_id={"tensor": other}, device_id_type=MESH)
    pl.semaphore_wait(barrier, 6)


def gather_kernel(vec_ref, qkv_ref, vec_out, qkv_out, vec_other, send, recv, local):
    along, x_way, y_way = partners_of(lax.axis_index("dp"))
    other = 1 - lax.axis_index("tensor")
    greet(along, x_way, y_way, other)
    blocks, outs = (vec_ref, qkv_ref), (vec_out, qkv_out)
    copies = {}

    def start(kind, source, slot, device):
        copy = pltpu.make_async_remote_copy(
            src_ref=source,
            dst_ref=outs[kind].at[slot],
            send_sem=send.at[kind, slot],
            recv_sem=recv.at[kind, slot],
            device_id={"dp": device},
            device_id_type=MESH,
        )
        copy.start()
        copies[kind, slot] = copy

    kept = []
    for kind in range(2):
        for step in range(1, 4):
            start(kind, blocks[kind], step, along[step - 1])
        start(kind, blocks[kind], 4, y_way)
        start(kind, blocks[kind], 8, x_way)
        copy = pltpu.make_async_copy(blocks[kind], outs[kind].at[0], local.at[kind])
        copy.start()
        kept.append(copy)
    for step in range(1, 4):
        for kind in range(2):
            copies[kind, step].wait_recv()
            start(kind, outs[kind].at[step], 4 + step, y_way)
            start(kind, outs[kind].at[step], 8 + step, x_way)
        if step == 1:
            for kind in range(2):
                copies[kind, 4].wait_recv()
                start(kind, outs[kind].at[4], 12, x_way)
    for step in range(1, 4):
        for kind in range(2):
            slot = 4 + step if step < 2 else 8 + step
            copies[kind, slot].wait_recv()
            start(kind, outs[kind].at[slot], 12 + step, x_way if step < 2 else y_way)
    waited = (1, 2, 3, 4, 5, 10, 11)
    rest = [slot for slot in range(4, 16) if slot not in waited]
    for slot in rest:
        copies[0, slot].wait_recv()
    kept[0].wait()
    shared = pltpu.make_async_remote_copy(
        src_ref=vec_out,
        dst_ref=vec_other,
        send_sem=send.at[0, 0],
        recv_sem=recv.at[0, 0],
        device_id={"tensor": other},
        device_id_type=MESH,
    )
    shared.start()
    for slot in rest:
        copies[1, slot].wait_recv()
    kept[1].wait()
    for copy in copies.values():
        copy.wait_send()
    shared.wait()


def gather_first(vectors, qkv):
    anywhere = pl.BlockSpec(memory_space=pl.ANY)
    inside = pl.BlockSpec(memory_space=pltpu.VMEM)
    return pl.pallas_call(
        gather_kernel,
        out_shape=(
            jax.ShapeDtypeStruct((16, *vectors.shape), vectors.dtype),
            jax.ShapeDtypeStruct((16, *qkv.shape), qkv.dtype),
            jax.ShapeDtypeStruct((16, *vectors.shape), vectors.dtype),
        ),
        in_specs=[inside, inside],
        out_specs=(anywhere, anywhere, anywhere),
        scratch_shapes=[
            pltpu.SemaphoreType.DMA((2, 16)),
            pltpu.SemaphoreType.DMA((2, 16)),
            pltpu.SemaphoreType.DMA((2,)),
        ],
        compiler_params=pltpu.CompilerParams(collective_id=0, has_side_effects=True),
        name="gather_first",
    )(vectors, qkv)


def scatter_kernel(
    small_ref, grad_ref, small_out, grad_out,
    small_via, small_fold, small_cross, small_sums, small_last,
    grad_via, grad_fold, grad_cross, grad_sums, grad_last,
    send, recv,
):
    along, x_way, y_way = partners_of(lax.axis_index("dp"))
    greet(along, x_way, y_way, 1 - lax.axis_index("tensor"))
    blocks, results = (small_ref, grad_ref), (small_out, grad_out)
    via, fold = (small_via, grad_via), (small_fold, grad_fold)
    cross, sums, last = (small_cross, grad_cross), (small_sums, grad_sums), (small_last, grad_last)
    copies = {}

    def start(kind, source, target, number, device):
        copy = pltpu.make_async_remote_copy(
            src_ref=source,
            dst_ref=target,
            send_sem=send.at[kind, number],
            recv_sem=recv.at[kind, number],
            device_id={"dp": device},
            device_id_type=MESH,
        )
        copy.start()
        copies[kind, number] = copy

    for kind in range(2):
        for step in range(4):
            way = x_way if step < 2 else y_way
            start(kind, blocks[kind].at[12 + step], via[kind].at[step], step, way)
    for kind in range(2):
        for step in range(2):
            start(kind, blocks[kind].at[6 + step], cross[kind].at[2 + step], 6 + step, y_way)
            start(kind, blocks[kind].at[8 + step], cross[kind].at[4 + step], 8 + step, x_way)
    for step in (1, 3, 0, 2):
        for kind in range(2):
            slot = 4 + step if step < 2 else 8 + step
            copies[kind, step].wait_recv()
            folded = blocks[kind][slot].astype(F32) + via[kind][step].astype(F32)
            fold[kind][step] = folded.astype(fold[kind].dtype)
            start(kind, fold[kind].at[step], cross[kind].at[slot - 4], slot, y_way if step < 2 else x_way)
    for step in (3, 1, 2, 0):
        for kind in range(2):
            copies[kind, 4 + step].wait_recv()
            copies[kind, 8 + step].wait_recv()
            total = blocks[kind][step].astype(F32)
            total = total + cross[kind][step].astype(F32) + cross[kind][4 + step].astype(F32)
            if step:
                sums[kind][step] = total.astype(sums[kind].dtype)
                start(kind, sums[kind].at[step], last[kind].at[step], 12 + step, along[3 - step])
            else:
                results[kind][...] = total
    for kind in range(2):
        for step in range(1, 4):
            copies[kind, 12 + step].wait_recv()
            results[kind][...] += last[kind][step].astype(F32)
    for copy in copies.values():
        copy.wait_send()


def scatter_last(small, grads):
    inside = pl.BlockSpec(memory_space=pltpu.VMEM)
    scratch = []
    for value in (small, grads):
        for slots in (4, 4, 8, 4, 4):
            scratch.append(pltpu.VMEM((slots, *value.shape[1:]), value.dtype))
    return pl.pallas_call(
        scatter_kernel,
        out_shape=(
            jax.ShapeDtypeStruct(small.shape[1:], F32),
            jax.ShapeDtypeStruct(grads.shape[1:], F32),
        ),
        in_specs=[inside, inside],
        out_specs=(inside, inside),
        scratch_shapes=scratch
        + [pltpu.SemaphoreType.DMA((2, 16)), pltpu.SemaphoreType.DMA((2, 16))],
        compiler_params=pltpu.CompilerParams(collective_id=1, has_side_effects=True),
        name="scatter_last",
    )(small, grads)


def swap(value):
    return lax.ppermute(value, "tensor", [(0, 1), (1, 0)])


def after(value, earlier):
    return lax.optimization_barrier((value, earlier))[0]


def dot(a, b):
    return lax.dot_general(a, b, (((1,), (0,)), ((), ())), preferred_element_type=F32)


def dot_nt(a, b):
    return lax.dot_general(a, b, (((1,), (1,)), ((), ())), preferred_element_type=F32)


def dot_tn(a, b):
    return lax.dot_general(a, b, (((0,), (0,)), ((), ())), preferred_element_type=F32)


def norm_parts(features):
    average = jnp.mean(features, axis=-1, keepdims=True)
    centered = features - average
    spread = jnp.mean(centered * centered, axis=-1, keepdims=True)
    scale = lax.rsqrt(spread + EPS)
    return centered * scale, scale


def norm_back(grad, normed, scale, gain):
    h = grad * gain
    return scale * (
        h - jnp.mean(h, axis=-1, keepdims=True) - normed * jnp.mean(h * normed, axis=-1, keepdims=True)
    )


def allowed_mask(first_query, query_count, key_count, prefix_length):
    query_pos = first_query + jnp.arange(query_count, dtype=jnp.int32)
    key_pos = jnp.arange(key_count, dtype=jnp.int32)
    return (key_pos[None, :] <= query_pos[:, None]) | (key_pos[None, :] < prefix_length)


def block_scores(query_rows, seq_keys, allowed, score_scale):
    scores = (
        jnp.einsum("qhd,khd->hqk", query_rows, seq_keys, preferred_element_type=F32)
        * score_scale
    )
    return jnp.where(allowed[None], scores, NEGATIVE)


def attention_pieces(length, heads_local):
    half, few = length // 2, heads_local // 2
    return [(0, half, 0, heads_local), (half, length, 0, few), (half, length, few, heads_local)]


def head_rows(rows, first_head, end_head, head_dim):
    return rows[:, first_head * head_dim : end_head * head_dim].reshape(
        rows.shape[0], end_head - first_head, head_dim
    )


def attention_forward(queries, keys_all, values_all, prefix, heads_local, head_dim, gates):
    outputs, logsums = [], []
    for number, piece in enumerate(attention_pieces(queries.shape[0], heads_local)):
        output, logsum = forward_piece(
            piece, after(queries, gates[number]), keys_all, values_all, prefix, head_dim
        )
        outputs.append(output)
        logsums.append(logsum)
    lower = jnp.concatenate(outputs[1:], axis=1)
    return (jnp.concatenate([outputs[0], lower], axis=0), logsums)


def forward_piece(piece, queries, keys_all, values_all, prefix, head_dim):
    first_row, reach, first_head, end_head = piece
    rows = reach - first_row
    seq_keys = head_rows(keys_all[:reach], first_head, end_head, head_dim)
    seq_values = head_rows(values_all[:reach], first_head, end_head, head_dim)
    query_rows = head_rows(queries[first_row:reach], first_head, end_head, head_dim)
    allowed = allowed_mask(first_row, rows, reach, prefix[0])
    scores = block_scores(query_rows, seq_keys, allowed, head_dim ** (-0.5))
    top_score = jnp.max(scores, axis=-1, keepdims=True)
    powered = jnp.exp(scores - top_score)
    totals = jnp.sum(powered, axis=-1, keepdims=True)
    probabilities = (powered / totals).astype(BF)
    attended = jnp.einsum("hqk,khd->qhd", probabilities, seq_values, preferred_element_type=F32)
    return (
        attended.reshape(rows, (end_head - first_head) * head_dim).astype(BF),
        top_score + jnp.log(totals),
    )


def attention_backward(
    queries, keys_all, values_all, prefix, logsums, back_attended, heads_local, head_dim, gates
):
    length = queries.shape[0]
    parts = []
    for number, piece in enumerate(attention_pieces(length, heads_local)):
        parts.append(
            backward_piece(
                piece,
                queries,
                keys_all,
                values_all,
                prefix,
                logsums[number],
                after(back_attended, gates[number]),
                head_dim,
            )
        )
    upper, lower = parts[0], [jnp.concatenate([a, b], axis=1) for a, b in zip(*parts[1:])]
    half = length // 2
    back_queries = jnp.concatenate([upper[0], lower[0]], axis=0)
    back_keys = jnp.concatenate([lower[1][:half] + upper[1], lower[1][half:]], axis=0)
    back_values = jnp.concatenate([lower[2][:half] + upper[2], lower[2][half:]], axis=0)
    return jnp.concatenate([back_queries, back_keys, back_values], axis=1).astype(BF)


def backward_piece(piece, queries, keys_all, values_all, prefix, logsum, back_attended, head_dim):
    score_scale = head_dim ** (-0.5)
    first_row, reach, first_head, end_head = piece
    rows = reach - first_row
    part = (end_head - first_head) * head_dim
    seq_keys = head_rows(keys_all[:reach], first_head, end_head, head_dim)
    seq_values = head_rows(values_all[:reach], first_head, end_head, head_dim)
    query_rows = head_rows(queries[first_row:reach], first_head, end_head, head_dim)
    back_rows = head_rows(back_attended[first_row:reach], first_head, end_head, head_dim)
    allowed = allowed_mask(first_row, rows, reach, prefix[0])
    scores = block_scores(query_rows, seq_keys, allowed, score_scale)
    probabilities = jnp.exp(scores - logsum)
    back_probs = jnp.einsum("qhd,khd->hqk", back_rows, seq_values, preferred_element_type=F32)
    row_dot = jnp.sum(probabilities * back_probs, axis=-1, keepdims=True)
    back_scores = (probabilities * (back_probs - row_dot)).astype(BF)
    back_query = (
        jnp.einsum("hqk,khd->qhd", back_scores, seq_keys, preferred_element_type=F32) * score_scale
    )
    back_key = (
        jnp.einsum("hqk,qhd->khd", back_scores, query_rows, preferred_element_type=F32) * score_scale
    )
    back_value = jnp.einsum(
        "hqk,qhd->khd", probabilities.astype(BF), back_rows, preferred_element_type=F32
    )
    return back_query.reshape(rows, part), back_key.reshape(reach, part), back_value.reshape(reach, part)


def body(
    ring,
    tokens,
    cotangent,
    prefix,
    routes,
    norm1_gain,
    norm1_bias,
    w_query,
    w_key,
    w_value,
    w_out,
    norm2_gain,
    norm2_bias,
    centroids,
    expert_in,
    expert_out,
):
    side = lax.axis_index("tensor")
    own_rows, width = tokens.shape
    all_rows = 2 * own_rows
    head_dim = width // HEADS
    heads_local = w_query.shape[1] // head_dim
    part = w_query.shape[1]
    rows = w_query.shape[0]
    experts, _, hidden = expert_in.shape
    count = ring.count

    def both(own):
        other = swap(own)
        return jnp.where(
            side == 0, jnp.concatenate([own, other], 0), jnp.concatenate([other, own], 0)
        )

    vectors = jnp.concatenate(
        [
            norm1_gain[None],
            norm1_bias[None],
            norm2_gain[None],
            norm2_bias[None],
            centroids,
        ],
        axis=0,
    )
    small_count = vectors.shape[0]
    qkv_block = jnp.concatenate([w_query, w_key, w_value, w_out.T], axis=1)
    in_block = expert_in.transpose(1, 0, 2).reshape(rows, experts * hidden)
    out_block = expert_out.transpose(2, 0, 1).reshape(rows, experts * hidden)
    if count == 16:
        padded = jnp.pad(vectors, ((0, 8 - small_count), (0, 128 - rows // 2)))
        table, qkv_w, other_table = gather_first(padded, qkv_block)
        table, other_table = (t[:, :small_count, : rows // 2] for t in (table, other_table))
        table = jnp.where(
            side == 0,
            jnp.concatenate([table, other_table], 2),
            jnp.concatenate([other_table, table], 2),
        )
        qkv_w = qkv_w.reshape(width, 4 * part)
    else:
        other_vectors = swap(vectors)
        vectors = jnp.where(
            side == 0,
            jnp.concatenate([vectors, other_vectors], 1),
            jnp.concatenate([other_vectors, vectors], 1),
        )
        table = ring.gather(vectors.reshape(1, small_count * rows)).reshape(count, small_count, rows)
        qkv_w = ring.gather(qkv_block)
    table = table.transpose(1, 0, 2).reshape(small_count, width)
    gain_one, bias_one, gain_two, bias_two = (table[i : i + 1] for i in range(4))
    centres = table[4:]

    qkv_w, in_block = lax.optimization_barrier((qkv_w, in_block))
    qkv_w, out_w = qkv_w[:, : 3 * part], qkv_w[:, 3 * part :]
    in_lead = ring.lead(in_block)
    in_crossed = ring.cross(in_lead)
    out_lead = ring.lead(after(out_block, in_lead))
    in_w = ring.close(in_lead, in_crossed)
    out_crossed = ring.cross(after(out_lead, in_w))
    back_w = ring.close(out_lead, out_crossed)

    found = ring.width_order(width)
    to_order = (jnp.arange(width, dtype=jnp.int32)[:, None] == found[None, :]).astype(BF)
    tokens_all = dot(both(tokens), to_order)
    back_all = lax.optimization_barrier(dot(both(cotangent), to_order).astype(BF)).astype(F32)

    normed_one, scale_one = norm_parts(tokens_all)
    first_rows = (normed_one * gain_one + bias_one).astype(BF)
    qkv = dot(first_rows, qkv_w).astype(BF)
    queries, keys_all, values_all = qkv[:, :part], qkv[:, part : 2 * part], qkv[:, 2 * part :]
    attended, logsums = attention_forward(
        queries, keys_all, values_all, prefix, heads_local, head_dim, [(), in_lead, ()]
    )
    attended = after(attended, (in_crossed, out_lead))
    attn_terms = dot_nt(attended, out_w).astype(BF)
    residual = tokens_all + (attn_terms.astype(F32) + swap(attn_terms).astype(F32))
    normed_two, scale_two = norm_parts(residual)
    second_rows = (normed_two * gain_two + bias_two).astype(BF)
    second_wide = second_rows.astype(F32)

    is_last = routes == 1
    ones_before = jnp.tril(jnp.ones((all_rows, all_rows), BF))
    last_before = dot(ones_before, is_last.astype(BF)).astype(jnp.int32)
    position = jnp.arange(all_rows, dtype=jnp.int32)[:, None]
    first_count = all_rows - last_before[all_rows - 1, 0]
    place = jnp.where(is_last, first_count + last_before - 1, position - last_before)
    sort_to = (place == jnp.arange(all_rows, dtype=jnp.int32)[None, :]).astype(BF)
    tail = all_rows - CAP
    in_first = position < first_count

    centre_rows = jnp.where(is_last, centres[1:2], centres[0:1])
    gate = jax.nn.sigmoid(jnp.sum(second_wide * centre_rows, axis=-1, keepdims=True))
    back_branch = (gate * back_all).astype(BF)
    gate, back_branch, sent_rows = lax.optimization_barrier((gate, back_branch, second_rows))
    picked = dot_tn(sort_to, sent_rows).astype(BF)
    back_slots = dot_tn(sort_to, back_branch).astype(BF)
    windows = (slice(0, CAP), slice(tail, all_rows))
    masks = (in_first[:CAP], ~in_first[tail:])
    slot_out, back_picked, grads_in, grads_out = [], [], [], []
    hidden_of = []
    for e in range(2):
        columns = slice(e * hidden, (e + 1) * hidden)
        rows_in = picked[windows[e]]
        back_rows = jnp.where(masks[e], back_slots[windows[e]], jnp.zeros((), BF))
        up = dot(rows_in, in_w[:, columns])
        activated = lax.optimization_barrier(jax.nn.gelu(up).astype(BF))
        grads_out.append(dot_tn(back_rows, activated).astype(BF))
        hidden_of.append((columns, rows_in, back_rows, up, activated))
    grads_out = jnp.concatenate(grads_out, axis=1)
    out_via = ring.far(grads_out, BF)
    for e, (columns, rows_in, back_rows, up, activated) in enumerate(hidden_of):
        if e == 1:
            back_rows = after(back_rows, out_via)
        slot_out.append(dot_nt(activated, back_w[:, columns]).astype(BF))
        back_activated = dot(back_rows, back_w[:, columns])
        back_up = jax.vjp(jax.nn.gelu, up)[1](back_activated)[0].astype(BF)
        grads_in.append(dot_tn(rows_in, back_up).astype(BF))
        back_picked.append(dot_nt(back_up, in_w[:, columns]).astype(BF))
    grads_in = jnp.concatenate(grads_in, axis=1)
    out_near = ring.near(grads_out, out_via, BF)
    in_via = ring.far(after(grads_in, out_via), BF)

    def unsort(pieces):
        joined = jnp.concatenate(
            [
                pieces[0][:tail],
                jnp.where(in_first[tail:CAP], pieces[0][tail:], pieces[1][: CAP - tail]),
                pieces[1][CAP - tail :],
            ],
            axis=0,
        )
        return dot(sort_to, joined).astype(BF)

    row_terms = unsort(slot_out)
    expert_rows = row_terms.astype(F32) + swap(row_terms).astype(F32)
    block_all = (residual + gate * expert_rows).astype(BF)
    first_own = side * own_rows
    block_out = dot_nt(lax.dynamic_slice_in_dim(block_all, first_own, own_rows), to_order).astype(BF)
    back_score = jnp.sum(back_all * expert_rows, axis=-1, keepdims=True) * gate * (1.0 - gate)

    second_terms = unsort(back_picked)
    back_second = second_terms.astype(F32) + swap(second_terms).astype(F32) + back_score * centre_rows
    weighted = back_score * second_wide
    grad_centre = jnp.stack(
        [
            jnp.sum(jnp.where(is_last, 0.0, weighted), axis=0),
            jnp.sum(jnp.where(is_last, weighted, 0.0), axis=0),
        ]
    )
    grad_gain_two = jnp.sum(back_second * normed_two, axis=0)
    grad_bias_two = jnp.sum(back_second, axis=0)
    back_residual = back_all + norm_back(back_second, normed_two, scale_two, gain_two)
    back_out = back_residual.astype(BF)
    grads_out = ring.last(grads_out, out_near, BF)
    in_near = ring.near(grads_in, in_via, BF)
    back_attended = dot(back_out, out_w).astype(BF)
    grad_out = dot_tn(back_out, attended).astype(BF)
    back_qkv = attention_backward(
        queries, keys_all, values_all, prefix, logsums, back_attended, heads_local, head_dim,
        [(), (out_near, in_via), ()],
    )
    back_qkv = after(back_qkv, (in_near, grads_out))
    grads_in = ring.last(grads_in, in_near, BF)
    grad_qkv = dot_tn(first_rows, back_qkv).astype(BF)
    first_terms = dot_nt(back_qkv, qkv_w).astype(BF)
    own_terms = lax.dynamic_slice_in_dim(first_terms, first_own, own_rows)
    other_terms = lax.dynamic_slice_in_dim(first_terms, own_rows - first_own, own_rows)
    back_first = own_terms.astype(F32) + swap(other_terms).astype(F32)

    def mine(value):
        return lax.dynamic_slice_in_dim(value, first_own, own_rows)

    normed_own = mine(normed_one)
    back_norm_one = norm_back(back_first, normed_own, mine(scale_one), gain_one)
    grad_tokens = dot_nt(
        (mine(back_residual) + back_norm_one).astype(BF), to_order
    ).astype(BF)
    one_part = jnp.stack([jnp.sum(back_first * normed_own, axis=0), jnp.sum(back_first, axis=0)])
    one_part = one_part + swap(one_part)
    small = jnp.concatenate(
        [one_part, grad_gain_two[None], grad_bias_two[None], grad_centre], axis=0
    )
    small = small.reshape(small_count, count, rows).transpose(1, 0, 2)
    grad_first = jnp.concatenate([grad_qkv, grad_out], axis=1)
    if count == 16:
        small = jnp.pad(small, ((0, 0), (0, 8 - small_count), (0, 128 - rows)))
        small, grad_first = scatter_last(small, grad_first.reshape(count, rows, 4 * part))
        small = small[:small_count, :rows]
    else:
        grad_first = ring.scatter(grad_first, BF)
        small = ring.scatter(small.reshape(count, small_count * rows), F32).reshape(small_count, rows)
    grad_qkv, grad_out = grad_first[:, : 3 * part], grad_first[:, 3 * part :]
    small = lax.dynamic_slice_in_dim(small, side * (rows // 2), rows // 2, axis=1)
    return (
        block_out,
        grad_tokens,
        small[0],
        small[1],
        grad_qkv[:, :part],
        grad_qkv[:, part : 2 * part],
        grad_qkv[:, 2 * part :],
        grad_out.T,
        small[2],
        small[3],
        small[4:],
        grads_in.reshape(rows, experts, hidden).transpose(1, 0, 2),
        grads_out.reshape(rows, experts, hidden).transpose(1, 2, 0),
    )


def solution(mesh):
    ring = Ring(mesh.shape["dp"])
    both, rows = P(("dp", "tensor")), P(("dp", "tensor"), None)
    columns = P("dp", "tensor")

    def step(*arguments):
        return body(ring, *arguments)

    return jax.shard_map(
        step,
        mesh=mesh,
        in_specs=(
            rows,
            rows,
            P("dp"),
            P("dp", None),
            both,
            both,
            columns,
            columns,
            columns,
            P("tensor", "dp"),
            both,
            both,
            P(None, ("dp", "tensor")),
            P(None, "dp", "tensor"),
            P(None, "tensor", "dp"),
        ),
        out_specs=(
            rows,
            rows,
            both,
            both,
            columns,
            columns,
            columns,
            P("tensor", "dp"),
            both,
            both,
            P(None, ("dp", "tensor")),
            P(None, "dp", "tensor"),
            P(None, "tensor", "dp"),
        ),
        check_vma=False,
    )
```

profile of v0, /device:TPU:0, one launch (start us, length us, event | category | flops | bytes accessed | tf_op | source)
XLA Modules:
  0.0 490.0 jit_solution(8783830598679962019)
XLA Ops:
  4.6 34.5 %gather_first.1 = (f32[16,8,128]{2,1,0:T(8,128)}, bf16[16,48,1536]{2,1,0:T(8,128)(2,1)}, f32[16,8,128]{2,1,0:T(8,128)}) custom-call(f32[8,128]{1,0:T(8,128)} %pad.8.vec_ref, bf16[48,1536]{1,0:T(8,128)(2,1)} %pad_maximum_fusion.9.qkv_ref), custom_call_target="tpu_custom_call" | custom-call | tf_op jit(solution)/shard_map/gather_first/pallas_call | solution.py:225
  54.3 13.8 %collective-permute-done.1 = bf16[48,3072]{1,0:T(8,128)(2,1)S(1)} collective-permute-done((bf16[48,3072]{1,0:T(8,128)(2,1)S(1)}, bf16[48,3072]{1,0:T(8,128)(2,1)S(1)}, u32[]{:S(2)}, u32[]{:S(2)}) %collective-permute-start.1) | collective-permute-done | bytes 294944 | tf_op jit(solution)/shard_map/ppermute | solution.py:54
  75.0 23.2 %collective-permute-done.6 = bf16[48,3072]{1,0:T(8,128)(2,1)S(1)} collective-permute-done((bf16[48,3072]{1,0:T(8,128)(2,1)S(1)}, bf16[48,3072]{1,0:T(8,128)(2,1)S(1)}, u32[]{:S(2)}, u32[]{:S(2)}) %collective-permute-start.6) | collective-permute-done | bytes 294944 | tf_op jit(solution)/shard_map/ppermute | solution.py:54
  168.3 9.5 %collective-permute-done.11 = bf16[96,3072]{1,0:T(8,128)(2,1)S(1)} collective-permute-done((bf16[96,3072]{1,0:T(8,128)(2,1)S(1)}, bf16[96,3072]{1,0:T(8,128)(2,1)S(1)}, u32[]{:S(2)}, u32[]{:S(2)}) %collective-permute-start.11) | collective-permute-done | bytes 589856 | tf_op jit(solution)/shard_map/ppermute | solution.py:54
  187.8 4.2 multiply_convert_fusion.3
  192.0 4.2 multiply_convert_fusion.4
  211.8 10.5 %collective-permute-done.19 = bf16[96,3072]{1,0:T(8,128)(2,1)S(1)} collective-permute-done((bf16[96,3072]{1,0:T(8,128)(2,1)S(1)}, bf16[96,3072]{1,0:T(8,128)(2,1)S(1)}, u32[]{:S(2)}, u32[]{:S(2)}) %collective-permute-start.19) | collective-permute-done | bytes 589856 | tf_op jit(solution)/shard_map/ppermute | solution.py:54
  226.4 7.0 %collective-permute-done.15 = bf16[96,3072]{1,0:T(8,128)(2,1)S(1)} collective-permute-done((bf16[96,3072]{1,0:T(8,128)(2,1)S(1)}, bf16[96,3072]{1,0:T(8,128)(2,1)S(1)}, u32[]{:S(2)}, u32[]{:S(2)}) %collective-permute-start.15) | collective-permute-done | bytes 589856 | tf_op jit(solution)/shard_map/ppermute | solution.py:54
  238.5 5.6 %fusion.16 = bf16[640,1536]{1,0:T(8,128)(2,1)S(1)} fusion(f32[640,1536]{1,0:T(8,128)} %get-tuple-element.152, bf16[768,3072]{1,0:T(8,128)(2,1)S(1)} %constant_dynamic-update-slice_fusion.16, bf16[1024,768]{1,0:T(8,128)(2,1)S(1)} %fusion.90, pred[640]{0:T(1024)(128)(4,1)S(1)} %copy-done.83), kind=kOutput, calls=%fused_computation.56 | convolution fusion | flops 1530101760 | bytes 9241600 | tf_op jit(solution)/shard_map/dot_general | solution.py:333
  248.3 4.2 fusion.23
  266.4 11.5 %collective-permute-done.24 = bf16[96,3072]{1,0:T(8,128)(2,1)S(1)} collective-permute-done((bf16[96,3072]{1,0:T(8,128)(2,1)S(1)}, bf16[96,3072]{1,0:T(8,128)(2,1)S(1)}, u32[]{:S(2)}, u32[]{:S(2)}) %collective-permute-start.24) | collective-permute-done | bytes 589856 | tf_op jit(solution)/shard_map/ppermute | solution.py:54
  287.4 16.3 %collective-permute-done.27 = bf16[48,3072]{1,0:T(8,128)(2,1)S(1)} collective-permute-done((bf16[48,3072]{1,0:T(8,128)(2,1)S(1)}, bf16[48,3072]{1,0:T(8,128)(2,1)S(1)}, u32[]{:S(2)}, u32[]{:S(2)}) %collective-permute-start.27) | collective-permute-done | bytes 294944 | tf_op jit(solution)/shard_map/ppermute | solution.py:54
  306.2 4.6 fusion.34
  329.3 7.7 %fusion.37 = f32[3,64,1024]{2,1,0:T(8,128)} fusion(bf16[512,3,64]{0,2,1:T(8,128)(2,1)S(1)} %bitcast.216, f32[3,512,1024]{2,1,0:T(8,128)} %fusion.253, f32[3,512]{1,0:T(4,128)S(1)} %get-tuple-element.156, pred[512,1024]{1,0:T(8,128)(4,1)S(1)} %copy-done.12), kind=kOutput, calls=%fused_computation.93 | convolution fusion | flops 207618048 | bytes 7804928 | tf_op jit(solution)/shard_map/hqk,qhd->khd/dot_general | solution.py:462
  339.9 5.9 %multiply_reduce_fusion.1 = (f32[3,512]{1,0:T(4,128)S(1)}, f32[3,512]{1,0:T(4,128)S(1)}, f32[3,512,1024]{2,1,0:T(8,128)}) fusion(f32[3,512,1024]{2,1,0:T(8,128)S(1)} %bitcast.163, f32[3,512]{1,0:T(4,128)S(1)} %get-tuple-element.157, pred[512,1024]{1,0:T(8,128)(4,1)S(1)} %copy-done.12, f32[3,512,1024]{2,1,0:T(8,128)S(1)} %fusion.254, ...), kind=kOutput, calls=%fused_computation.15 | convolution fusion | flops 217052160 | bytes 26304512 | tf_op jit(solution)/shard_map/qhd,khd->hqk/dot_general | solution.py:453
  345.8 7.9 %multiply_convert_fusion.1 = (bf16[3,512,1024]{2,1,0:T(8,128)(2,1)}, bf16[3,512,1024]{2,1,0:T(8,128)(2,1)S(1)}) fusion(f32[3,512,1024]{2,1,0:T(8,128)} %get-tuple-element.153, f32[3,512,1024]{2,1,0:T(8,128)S(1)} %bitcast.163, f32[3,512]{1,0:T(4,128)S(1)} %get-tuple-element.59, f32[3,512]{1,0:T(4,128)S(1)} %get-tuple-element.157, ...), kind=kLoop, calls=%fused_computation.14 | loop fusion | flops 18874368 | bytes 32006144 | tf_op jit(solution)/shard_map/convert_element_type | solution.py:455
  364.3 5.6 %fusion.35 = f32[6,64,512]{2,1,0:T(8,128)} fusion(bf16[512,6,64]{0,2,1:T(8,128)(2,1)} %bitcast.200, f32[6,512,512]{1,2,0:T(8,128)} %fusion.251, f32[6,512]{1,0:T(8,128)S(1)} %copy-done.58, pred[512,512]{0,1:T(8,128)(4,1)S(1)} %copy-done.18), kind=kOutput, calls=%fused_computation.92 | convolution fusion | flops 207618048 | bytes 7745536 | tf_op jit(solution)/shard_map/hqk,qhd->khd/dot_general | solution.py:462
  369.9 7.7 %multiply_reduce_fusion.2 = (f32[6,512]{1,0:T(8,128)S(1)}, f32[6,512,512]{1,2,0:T(8,128)}) fusion(f32[6,512,512]{1,2,0:T(8,128)} %fusion.251, f32[6,512]{1,0:T(8,128)S(1)} %copy-done.58, pred[512,512]{0,1:T(8,128)(4,1)S(1)} %copy-done.18, bf16[512,6,64]{0,2,1:T(8,128)(2,1)S(1)} %bitcast.201, bf16[512,6,64]{0,2,1:T(8,128)(2,1)S(1)} %bitcast.199), kind=kOutput, calls=%fused_computation.18 | convolution fusion | flops 209187840 | bytes 13656064 | tf_op jit(solution)/shard_map/qhd,khd->hqk/dot_general | solution.py:453
  377.6 4.7 multiply_convert_fusion.2
  396.6 8.8 %maximum_maximum_fusion = bf16[1024,1152]{0,1:T(8,128)(2,1)S(1)} fusion(bf16[512,384]{0,1:T(8,128)(2,1)S(1)} %copy-done.37, bf16[512,384]{0,1:T(8,128)(2,1)S(1)} %fusion.161, bf16[512,384]{0,1:T(8,128)(2,1)S(1)} %fusion.167, bf16[512,384]{0,1:T(8,128)(2,1)S(1)} %copy-done.36, bf16[512,192]{0,1:T(8,128)(2,1)S(1)} %bitcast.213, ...), kind=kLoop, calls=%fused_computation.112 | loop fusion | flops 16515072 | bytes 4718592 | tf_op jit(solution)/shard_map/concatenate | solution.py:438
  412.4 6.1 %collective-permute-start.32 = (bf16[48,3072]{1,0:T(8,128)(2,1)S(1)}, bf16[48,3072]{1,0:T(8,128)(2,1)S(1)}, u32[]{:S(2)}, u32[]{:S(2)}) collective-permute-start(bf16[48,3072]{1,0:T(8,128)(2,1)S(1)} %get-tuple-element.106), channel_id=1, source_target_pairs={{0,16},{2,18},{4,20},{6,22},{8,0},{10,2},{12,4},{14,6},{16,24},{18... | collective-permute-start | bytes 884744 | tf_op jit(solution)/shard_map/ppermute | solution.py:54
  426.0 8.3 %collective-permute-done.34 = bf16[48,3072]{1,0:T(8,128)(2,1)S(1)} collective-permute-done((bf16[48,3072]{1,0:T(8,128)(2,1)S(1)}, bf16[48,3072]{1,0:T(8,128)(2,1)S(1)}, u32[]{:S(2)}, u32[]{:S(2)}) %collective-permute-start.34) | collective-permute-done | bytes 294944 | tf_op jit(solution)/shard_map/ppermute | solution.py:54
  434.3 5.5 %collective-permute-done.33 = bf16[48,3072]{1,0:T(8,128)(2,1)S(1)} collective-permute-done((bf16[48,3072]{1,0:T(8,128)(2,1)S(1)}, bf16[48,3072]{1,0:T(8,128)(2,1)S(1)}, u32[]{:S(2)}, u32[]{:S(2)}) %collective-permute-start.33) | collective-permute-done | bytes 294944 | tf_op jit(solution)/shard_map/ppermute | solution.py:54
  444.8 41.1 %scatter_last.1 = (f32[8,128]{1,0:T(8,128)}, f32[48,1536]{1,0:T(8,128)}) custom-call(f32[16,8,128]{2,1,0:T(8,128)} %pad.9.small_ref, bf16[16,48,1536]{2,1,0:T(8,128)(2,1)} %bitcast.166), custom_call_target="tpu_custom_call" | custom-call | tf_op jit(solution)/shard_map/scatter_last/pallas_call | solution.py:309
  (446 shorter events, 227.4 us)
Async XLA Ops:
  39.0 30.8 %collective-permute-start.3 = (bf16[48,3072]{1,0:T(8,128)(2,1)S(1)}, bf16[48,3072]{1,0:T(8,128)(2,1)S(1)}, u32[]{:S(2)}, u32[]{:S(2)}) collective-permute-start(bf16[48,3072]{1,0:T(8,128)(2,1)S(1)} %bitcast.202), channel_id=1, source_target_pairs={{0,16},{2,18},{4,20},{6,22},{8,0},{10,2},{12,4},{14,6},{16,24},{18... | collective-permute-start | bytes 884744 | tf_op jit(solution)/shard_map/ppermute | solution.py:54
  41.5 27.4 %collective-permute-start.2 = (bf16[48,3072]{1,0:T(8,128)(2,1)S(1)}, bf16[48,3072]{1,0:T(8,128)(2,1)S(1)}, u32[]{:S(2)}, u32[]{:S(2)}) collective-permute-start(bf16[48,3072]{1,0:T(8,128)(2,1)S(1)} %bitcast.203), channel_id=1, source_target_pairs={{0,24},{2,26},{4,28},{6,30},{8,16},{10,18},{12,20},{14,22},{16,8},... | collective-permute-start | bytes 884744 | tf_op jit(solution)/shard_map/ppermute | solution.py:54
  43.0 25.1 %collective-permute-start.1 = (bf16[48,3072]{1,0:T(8,128)(2,1)S(1)}, bf16[48,3072]{1,0:T(8,128)(2,1)S(1)}, u32[]{:S(2)}, u32[]{:S(2)}) collective-permute-start(bf16[48,3072]{1,0:T(8,128)(2,1)S(1)} %bitcast.204), channel_id=1, source_target_pairs={{0,8},{2,10},{4,12},{6,14},{8,24},{10,26},{12,28},{14,30},{16,0},{... | collective-permute-start | bytes 884744 | tf_op jit(solution)/shard_map/ppermute | solution.py:54
  43.0 60.7 %collective-permute-start = (bf16[512,768]{1,0:T(8,128)(2,1)}, bf16[512,768]{1,0:T(8,128)(2,1)S(1)}, u32[]{:S(2)}, u32[]{:S(2)}) collective-permute-start(bf16[512,768]{1,0:T(8,128)(2,1)} %param.15), channel_id=1, source_target_pairs={{0,1},{1,0},{2,3},{3,2},{4,5},{5,4},{6,7},{7,6},{8,9},{9,8},{10,11... | collective-permute-start | bytes 2359304 | tf_op jit(solution)/shard_map/ppermute | solution.py:325
  43.0 71.4 %collective-permute-start.10 = (bf16[512,768]{1,0:T(8,128)(2,1)}, bf16[512,768]{1,0:T(8,128)(2,1)}, u32[]{:S(2)}, u32[]{:S(2)}) collective-permute-start(bf16[512,768]{1,0:T(8,128)(2,1)} %param.16), channel_id=1, source_target_pairs={{0,1},{1,0},{2,3},{3,2},{4,5},{5,4},{6,7},{7,6},{8,9},{9,8},{10,11... | collective-permute-start | bytes 2359304 | tf_op jit(solution)/shard_map/ppermute | solution.py:325
  70.7 31.1 %collective-permute-start.8 = (bf16[48,3072]{1,0:T(8,128)(2,1)S(1)}, bf16[48,3072]{1,0:T(8,128)(2,1)S(1)}, u32[]{:S(2)}, u32[]{:S(2)}) collective-permute-start(bf16[48,3072]{1,0:T(8,128)(2,1)S(1)} %bitcast.206), channel_id=1, source_target_pairs={{0,16},{2,18},{4,20},{6,22},{8,0},{10,2},{12,4},{14,6},{16,24},{18... | collective-permute-start | bytes 884744 | tf_op jit(solution)/shard_map/ppermute | solution.py:54
  70.7 28.8 %collective-permute-start.7 = (bf16[48,3072]{1,0:T(8,128)(2,1)S(1)}, bf16[48,3072]{1,0:T(8,128)(2,1)S(1)}, u32[]{:S(2)}, u32[]{:S(2)}) collective-permute-start(bf16[48,3072]{1,0:T(8,128)(2,1)S(1)} %bitcast.207), channel_id=1, source_target_pairs={{0,24},{2,26},{4,28},{6,30},{8,16},{10,18},{12,20},{14,22},{16,8},... | collective-permute-start | bytes 884744 | tf_op jit(solution)/shard_map/ppermute | solution.py:54
  72.9 25.3 %collective-permute-start.6 = (bf16[48,3072]{1,0:T(8,128)(2,1)S(1)}, bf16[48,3072]{1,0:T(8,128)(2,1)S(1)}, u32[]{:S(2)}, u32[]{:S(2)}) collective-permute-start(bf16[48,3072]{1,0:T(8,128)(2,1)S(1)} %bitcast.208), channel_id=1, source_target_pairs={{0,8},{2,10},{4,12},{6,14},{8,24},{10,26},{12,28},{14,30},{16,0},{... | collective-permute-start | bytes 884744 | tf_op jit(solution)/shard_map/ppermute | solution.py:54
  98.2 60.5 %collective-permute-start.5 = (bf16[192,3072]{1,0:T(8,128)(2,1)}, bf16[192,3072]{1,0:T(8,128)(2,1)}, u32[]{:S(2)}, u32[]{:S(2)}) collective-permute-start(bf16[192,3072]{1,0:T(8,128)(2,1)} %get-tuple-element.127), channel_id=1, source_target_pairs={{0,4},{2,6},{4,0},{6,2},{8,12},{10,14},{12,8},{14,10},{16,20},{18,... | collective-permute-start | bytes 3538952 | tf_op jit(solution)/shard_map/ppermute | solution.py:54
  99.5 59.3 %collective-permute-start.4 = (bf16[192,3072]{1,0:T(8,128)(2,1)}, bf16[192,3072]{1,0:T(8,128)(2,1)}, u32[]{:S(2)}, u32[]{:S(2)}) collective-permute-start(bf16[192,3072]{1,0:T(8,128)(2,1)} %get-tuple-element.127), channel_id=1, source_target_pairs={{0,2},{2,0},{4,6},{6,4},{8,10},{10,8},{12,14},{14,12},{16,18},{18,... | collective-permute-start | bytes 3538952 | tf_op jit(solution)/shard_map/ppermute | solution.py:54
  160.8 21.6 %collective-permute-start.9 = (bf16[1024,768]{0,1:T(8,128)(2,1)S(1)}, bf16[1024,768]{0,1:T(8,128)(2,1)S(1)}, u32[]{:S(2)}, u32[]{:S(2)}) collective-permute-start(bf16[1024,768]{0,1:T(8,128)(2,1)S(1)} %convolution_convert_fusion.6), channel_id=1, source_target_pairs={{0,1},{1,0},{2,3},{3,2},{4,5},{5,4},{6,7},{7,6},{8,9},{9,8},{10,11... | collective-permute-start | bytes 4718600 | tf_op jit(solution)/shard_map/ppermute | solution.py:325
  179.3 28.8 %collective-permute-start.14 = (bf16[192,3072]{1,0:T(8,128)(2,1)S(1)}, bf16[192,3072]{1,0:T(8,128)(2,1)S(1)}, u32[]{:S(2)}, u32[]{:S(2)}) collective-permute-start(bf16[192,3072]{1,0:T(8,128)(2,1)S(1)} %copy-done.60), channel_id=1, source_target_pairs={{0,2},{2,0},{4,6},{6,4},{8,10},{10,8},{12,14},{14,12},{16,18},{18,... | collective-permute-start | bytes 3538952 | tf_op jit(solution)/shard_map/ppermute | solution.py:54
  180.9 28.9 %collective-permute-start.13 = (bf16[192,3072]{1,0:T(8,128)(2,1)S(1)}, bf16[192,3072]{1,0:T(8,128)(2,1)S(1)}, u32[]{:S(2)}, u32[]{:S(2)}) collective-permute-start(bf16[192,3072]{1,0:T(8,128)(2,1)S(1)} %copy-done.60), channel_id=1, source_target_pairs={{0,4},{2,6},{4,0},{6,2},{8,12},{10,14},{12,8},{14,10},{16,20},{18,... | collective-permute-start | bytes 3538952 | tf_op jit(solution)/shard_map/ppermute | solution.py:54
  208.2 26.8 %collective-permute-start.16 = (bf16[96,3072]{1,0:T(8,128)(2,1)S(1)}, bf16[96,3072]{1,0:T(8,128)(2,1)S(1)}, u32[]{:S(2)}, u32[]{:S(2)}) collective-permute-start(bf16[96,3072]{1,0:T(8,128)(2,1)S(1)} %slice.438), channel_id=1, source_target_pairs={{0,4},{2,6},{4,0},{6,2},{8,12},{10,14},{12,8},{14,10},{16,20},{18,... | collective-permute-start | bytes 1769480 | tf_op jit(solution)/shard_map/ppermute | solution.py:54
  210.0 23.4 %collective-permute-start.15 = (bf16[96,3072]{1,0:T(8,128)(2,1)S(1)}, bf16[96,3072]{1,0:T(8,128)(2,1)S(1)}, u32[]{:S(2)}, u32[]{:S(2)}) collective-permute-start(bf16[96,3072]{1,0:T(8,128)(2,1)S(1)} %slice.437), channel_id=1, source_target_pairs={{0,2},{2,0},{4,6},{6,4},{8,10},{10,8},{12,14},{14,12},{16,18},{18,... | collective-permute-start | bytes 1769480 | tf_op jit(solution)/shard_map/ppermute | solution.py:54
  224.3 56.2 %collective-permute-start.22 = (bf16[192,3072]{1,0:T(8,128)(2,1)}, bf16[192,3072]{1,0:T(8,128)(2,1)}, u32[]{:S(2)}, u32[]{:S(2)}) collective-permute-start(bf16[192,3072]{1,0:T(8,128)(2,1)} %get-tuple-element.89), channel_id=1, source_target_pairs={{0,4},{2,6},{4,0},{6,2},{8,12},{10,14},{12,8},{14,10},{16,20},{18,... | collective-permute-start | bytes 3538952 | tf_op jit(solution)/shard_map/ppermute | solution.py:54
  225.8 54.7 %collective-permute-start.21 = (bf16[192,3072]{1,0:T(8,128)(2,1)}, bf16[192,3072]{1,0:T(8,128)(2,1)}, u32[]{:S(2)}, u32[]{:S(2)}) collective-permute-start(bf16[192,3072]{1,0:T(8,128)(2,1)} %get-tuple-element.90), channel_id=1, source_target_pairs={{0,2},{2,0},{4,6},{6,4},{8,10},{10,8},{12,14},{14,12},{16,18},{18,... | collective-permute-start | bytes 3538952 | tf_op jit(solution)/shard_map/ppermute | solution.py:54
  261.2 45.0 %collective-permute-start.17 = (bf16[1024,768]{0,1:T(8,128)(2,1)}, bf16[1024,768]{0,1:T(8,128)(2,1)}, u32[]{:S(2)}, u32[]{:S(2)}) collective-permute-start(bf16[1024,768]{0,1:T(8,128)(2,1)} %fusion.93), channel_id=1, source_target_pairs={{0,1},{1,0},{2,3},{3,2},{4,5},{5,4},{6,7},{7,6},{8,9},{9,8},{10,11... | collective-permute-start | bytes 4718600 | tf_op jit(solution)/shard_map/ppermute | solution.py:325
  277.8 32.9 %collective-permute-start.20 = (bf16[1024,768]{0,1:T(8,128)(2,1)S(1)}, bf16[1024,768]{0,1:T(8,128)(2,1)S(1)}, u32[]{:S(2)}, u32[]{:S(2)}) collective-permute-start(bf16[1024,768]{0,1:T(8,128)(2,1)S(1)} %fusion.94), channel_id=1, source_target_pairs={{0,1},{1,0},{2,3},{3,2},{4,5},{5,4},{6,7},{7,6},{8,9},{9,8},{10,11... | collective-permute-start | bytes 4718600 | tf_op jit(solution)/shard_map/ppermute | solution.py:325
  282.8 21.0 %collective-permute-start.27 = (bf16[48,3072]{1,0:T(8,128)(2,1)S(1)}, bf16[48,3072]{1,0:T(8,128)(2,1)S(1)}, u32[]{:S(2)}, u32[]{:S(2)}) collective-permute-start(bf16[48,3072]{1,0:T(8,128)(2,1)S(1)} %get-tuple-element.109), channel_id=1, source_target_pairs={{0,16},{2,18},{4,20},{6,22},{8,0},{10,2},{12,4},{14,6},{16,24},{18... | collective-permute-start | bytes 884744 | tf_op jit(solution)/shard_map/ppermute | solution.py:54
  282.8 20.9 %collective-permute-start.29 = (bf16[48,3072]{1,0:T(8,128)(2,1)S(1)}, bf16[48,3072]{1,0:T(8,128)(2,1)S(1)}, u32[]{:S(2)}, u32[]{:S(2)}) collective-permute-start(bf16[48,3072]{1,0:T(8,128)(2,1)S(1)} %get-tuple-element.110), channel_id=1, source_target_pairs={{0,8},{2,10},{4,12},{6,14},{8,24},{10,26},{12,28},{14,30},{16,0},{... | collective-permute-start | bytes 884744 | tf_op jit(solution)/shard_map/ppermute | solution.py:54
  303.7 101.8 %collective-permute-start.25 = (bf16[192,3072]{1,0:T(8,128)(2,1)}, bf16[192,3072]{1,0:T(8,128)(2,1)}, u32[]{:S(2)}, u32[]{:S(2)}) collective-permute-start(bf16[192,3072]{1,0:T(8,128)(2,1)} %pad_maximum_fusion.3), channel_id=1, source_target_pairs={{0,2},{2,0},{4,6},{6,4},{8,10},{10,8},{12,14},{14,12},{16,18},{18,... | collective-permute-start | bytes 3538952 | tf_op jit(solution)/shard_map/ppermute | solution.py:54
  303.7 101.8 %collective-permute-start.26 = (bf16[192,3072]{1,0:T(8,128)(2,1)}, bf16[192,3072]{1,0:T(8,128)(2,1)}, u32[]{:S(2)}, u32[]{:S(2)}) collective-permute-start(bf16[192,3072]{1,0:T(8,128)(2,1)} %pad_maximum_fusion.4), channel_id=1, source_target_pairs={{0,4},{2,6},{4,0},{6,2},{8,12},{10,14},{12,8},{14,10},{16,20},{18,... | collective-permute-start | bytes 3538952 | tf_op jit(solution)/shard_map/ppermute | solution.py:54
  418.8 21.0 %collective-permute-start.33 = (bf16[48,3072]{1,0:T(8,128)(2,1)S(1)}, bf16[48,3072]{1,0:T(8,128)(2,1)S(1)}, u32[]{:S(2)}, u32[]{:S(2)}) collective-permute-start(bf16[48,3072]{1,0:T(8,128)(2,1)S(1)} %get-tuple-element.108), channel_id=1, source_target_pairs={{0,24},{2,26},{4,28},{6,30},{8,16},{10,18},{12,20},{14,22},{16,8},... | collective-permute-start | bytes 884744 | tf_op jit(solution)/shard_map/ppermute | solution.py:54
  (112 other events, 1193.3 us)
where the time goes:
time: 494 us; the launch traced here: 490 us
  matrix products  134 us (27%)
  waiting for transfers between devices  117 us (24%)
  Pallas kernels  75.6 us (15%)
  local copies, waits for them, and re-layouts  61.6 us (12%)
  other arithmetic  60.9 us (12%)
  starting transfers between devices  36.9 us (7%)
    ppermute x28, waiting for transfers between devices, move(): return lax.ppermute(value, 'dp', self.shift(stage, step))  117 us
    pallas_call x1, Pallas kernels, scatter_last(): pl.pallas_call(scatter_kernel, out_shape=(jax.ShapeDtypeStruct(small.shap...  41.1 us
    ppermute x28, starting transfers between devices, move(): return lax.ppermute(value, 'dp', self.shift(stage, step))  36.1 us
    dot_general x11, matrix products, dot(): lax.dot_general(a, b, (((1,), (0,)), ((), ())), preferred_element_type=F32)  34.8 us
    pallas_call x1, Pallas kernels, gather_first(): pl.pallas_call(gather_kernel, out_shape=(jax.ShapeDtypeStruct((16, *vecto...  34.5 us
    unnamed x210, local copies, waits for them, and re-layouts  17.6 us
    dot_general x6, matrix products, block_scores(): jnp.einsum('qhd,khd->hqk', query_rows, seq_keys, preferred_element_type=F32)  17.5 us
    dot_general x8, matrix products, dot_tn(): lax.dot_general(a, b, (((0,), (0,)), ((), ())), preferred_element_type=F32)  16.8 us
  transfers between devices with their start and end apart: 35, of which 14 were waited for; matrix products, arithmetic and copies ran while one was open for 47% of the time, Pallas kernels for 0%

commit v1 on v0

--- a/solution.py
+++ b/solution.py
@@ -1,3 +1,5 @@
+import functools
+
 import jax
 import jax.numpy as jnp
 from jax import lax
@@ -57,7 +59,7 @@
         for stage in range(len(self.sizes) - (2 if self.square else 0)):
             parts = [block] + [self.move(block, stage, s) for s in range(1, self.sizes[stage])]
             block = jnp.concatenate(parts, axis=0)
-        return block
+        return lax.optimization_barrier(block)
 
     def cross(self, block):
         if not self.square:
@@ -356,113 +358,112 @@
     )
 
 
-def allowed_mask(first_query, query_count, key_count, prefix_length):
-    query_pos = first_query + jnp.arange(query_count, dtype=jnp.int32)
-    key_pos = jnp.arange(key_count, dtype=jnp.int32)
-    return (key_pos[None, :] <= query_pos[:, None]) | (key_pos[None, :] < prefix_length)
-
-
-def block_scores(query_rows, seq_keys, allowed, score_scale):
-    scores = (
-        jnp.einsum("qhd,khd->hqk", query_rows, seq_keys, preferred_element_type=F32)
-        * score_scale
-    )
-    return jnp.where(allowed[None], scores, NEGATIVE)
-
-
-def attention_pieces(length, heads_local):
-    half, few = length // 2, heads_local // 2
-    return [(0, half, 0, heads_local), (half, length, 0, few), (half, length, few, heads_local)]
-
-
-def head_rows(rows, first_head, end_head, head_dim):
-    return rows[:, first_head * head_dim : end_head * head_dim].reshape(
-        rows.shape[0], end_head - first_head, head_dim
-    )
-
-
-def attention_forward(queries, keys_all, values_all, prefix, heads_local, head_dim, gates):
-    outputs, logsums = [], []
-    for number, piece in enumerate(attention_pieces(queries.shape[0], heads_local)):
-        output, logsum = forward_piece(
-            piece, after(queries, gates[number]), keys_all, values_all, prefix, head_dim
-        )
-        outputs.append(output)
-        logsums.append(logsum)
-    lower = jnp.concatenate(outputs[1:], axis=1)
-    return (jnp.concatenate([outputs[0], lower], axis=0), logsums)
-
-
-def forward_piece(piece, queries, keys_all, values_all, prefix, head_dim):
-    first_row, reach, first_head, end_head = piece
-    rows = reach - first_row
-    seq_keys = head_rows(keys_all[:reach], first_head, end_head, head_dim)
-    seq_values = head_rows(values_all[:reach], first_head, end_head, head_dim)
-    query_rows = head_rows(queries[first_row:reach], first_head, end_head, head_dim)
-    allowed = allowed_mask(first_row, rows, reach, prefix[0])
-    scores = block_scores(query_rows, seq_keys, allowed, head_dim ** (-0.5))
-    top_score = jnp.max(scores, axis=-1, keepdims=True)
-    powered = jnp.exp(scores - top_score)
-    totals = jnp.sum(powered, axis=-1, keepdims=True)
-    probabilities = (powered / totals).astype(BF)
-    attended = jnp.einsum("hqk,khd->qhd", probabilities, seq_values, preferred_element_type=F32)
-    return (
-        attended.reshape(rows, (end_head - first_head) * head_dim).astype(BF),
-        top_score + jnp.log(totals),
-    )
-
-
-def attention_backward(
-    queries, keys_all, values_all, prefix, logsums, back_attended, heads_local, head_dim, gates
+STRIP = 256
+
+
+def strip_scores(keys, queries, first, prefix):
+    scores = dot_nt(keys, queries) * (queries.shape[1] ** (-0.5))
+    key = lax.broadcasted_iota(jnp.int32, scores.shape, 0)
+    query = first + lax.broadcasted_iota(jnp.int32, scores.shape, 1)
+    return jnp.where((key <= query) | (key < prefix), scores, NEGATIVE)
+
+
+def strips(length):
+    return [(first, max(length // 2, first + STRIP)) for first in range(0, length, STRIP)]
+
+
+def attend_kernel(head_dim, prefix_ref, q_ref, k_ref, v_ref, out_ref, lse_ref):
+    prefix = prefix_ref[0]
+    for head in range(q_ref.shape[1] // head_dim):
+        columns = slice(head * head_dim, (head + 1) * head_dim)
+        for first, reach in strips(q_ref.shape[0]):
+            own = slice(first, first + STRIP)
+            scores = strip_scores(k_ref[:reach, columns], q_ref[own, columns], first, prefix)
+            top = jnp.max(scores, axis=0, keepdims=True)
+            powered = jnp.exp(scores - top)
+            total = jnp.sum(powered, axis=0, keepdims=True)
+            probabilities = (powered * (1.0 / total)).astype(BF)
+            attended = dot_tn(v_ref[:reach, columns], probabilities)
+            out_ref[own, columns] = attended.T.astype(BF)
+            lse_ref[0, head : head + 1, own] = top + jnp.log(total)
+
+
+def attend_back_kernel(
+    head_dim, prefix_ref, q_ref, k_ref, v_ref, back_ref, lse_ref, out_ref, key_sum, value_sum
 ):
-    length = queries.shape[0]
-    parts = []
-    for number, piece in enumerate(attention_pieces(length, heads_local)):
-        parts.append(
-            backward_piece(
-                piece,
-                queries,
-                keys_all,
-                values_all,
-                prefix,
-                logsums[number],
-                after(back_attended, gates[number]),
-                head_dim,
-            )
-        )
-    upper, lower = parts[0], [jnp.concatenate([a, b], axis=1) for a, b in zip(*parts[1:])]
-    half = length // 2
-    back_queries = jnp.concatenate([upper[0], lower[0]], axis=0)
-    back_keys = jnp.concatenate([lower[1][:half] + upper[1], lower[1][half:]], axis=0)
-    back_values = jnp.concatenate([lower[2][:half] + upper[2], lower[2][half:]], axis=0)
-    return jnp.concatenate([back_queries, back_keys, back_values], axis=1).astype(BF)
-
-
-def backward_piece(piece, queries, keys_all, values_all, prefix, logsum, back_attended, head_dim):
+    prefix = prefix_ref[0]
     score_scale = head_dim ** (-0.5)
-    first_row, reach, first_head, end_head = piece
-    rows = reach - first_row
-    part = (end_head - first_head) * head_dim
-    seq_keys = head_rows(keys_all[:reach], first_head, end_head, head_dim)
-    seq_values = head_rows(values_all[:reach], first_head, end_head, head_dim)
-    query_rows = head_rows(queries[first_row:reach], first_head, end_head, head_dim)
-    back_rows = head_rows(back_attended[first_row:reach], first_head, end_head, head_dim)
-    allowed = allowed_mask(first_row, rows, reach, prefix[0])
-    scores = block_scores(query_rows, seq_keys, allowed, score_scale)
-    probabilities = jnp.exp(scores - logsum)
-    back_probs = jnp.einsum("qhd,khd->hqk", back_rows, seq_values, preferred_element_type=F32)
-    row_dot = jnp.sum(probabilities * back_probs, axis=-1, keepdims=True)
-    back_scores = (probabilities * (back_probs - row_dot)).astype(BF)
-    back_query = (
-        jnp.einsum("hqk,khd->qhd", back_scores, seq_keys, preferred_element_type=F32) * score_scale
-    )
-    back_key = (
-        jnp.einsum("hqk,qhd->khd", back_scores, query_rows, preferred_element_type=F32) * score_scale
-    )
-    back_value = jnp.einsum(
-        "hqk,qhd->khd", probabilities.astype(BF), back_rows, preferred_element_type=F32
-    )
-    return back_query.reshape(rows, part), back_key.reshape(reach, part), back_value.reshape(reach, part)
+    for head in range(q_ref.shape[1] // head_dim):
+        columns = slice(head * head_dim, (head + 1) * head_dim)
+        for first, reach in reversed(strips(q_ref.shape[0])):
+            own = slice(first, first + STRIP)
+            keys, queries = k_ref[:reach, columns], q_ref[own, columns]
+            back_rows = back_ref[own, columns]
+            scores = strip_scores(keys, queries, first, prefix)
+            probabilities = jnp.exp(scores - lse_ref[0, head : head + 1, own])
+            back_probs = dot_nt(v_ref[:reach, columns], back_rows)
+            row_dot = jnp.sum(probabilities * back_probs, axis=0, keepdims=True)
+            back_scores = (probabilities * (back_probs - row_dot)).astype(BF)
+            out_ref[0, own, columns] = (dot_tn(keys, back_scores) * score_scale).T.astype(BF)
+            back_key = dot(back_scores, queries)
+            back_value = dot(probabilities.astype(BF), back_rows)
+            if reach == q_ref.shape[0]:
+                key_sum[...] = back_key
+                value_sum[...] = back_value
+            else:
+                key_sum[:reach, :] += back_key
+                value_sum[:reach, :] += back_value
+        out_ref[1, :, columns] = (key_sum[...] * score_scale).astype(BF)
+        out_ref[2, :, columns] = value_sum[...].astype(BF)
+
+
+def attend_specs(length, groups):
+    joint = [
+        pl.BlockSpec((length, 128), lambda i, kind=kind: (0, kind * groups + i)) for kind in range(3)
+    ]
+    rows = pl.BlockSpec((length, 128), lambda i: (0, i))
+    sums = pl.BlockSpec((1, 8, length), lambda i: (i, 0, 0))
+    return [pl.BlockSpec(memory_space=pltpu.SMEM)] + joint, rows, sums
+
+
+def attend(qkv, prefix, head_dim):
+    length, part = qkv.shape[0], qkv.shape[1] // 3
+    groups = part // 128
+    inputs, rows, sums = attend_specs(length, groups)
+    work = length * length * part
+    return pl.pallas_call(
+        functools.partial(attend_kernel, head_dim),
+        grid=(groups,),
+        out_shape=(
+            jax.ShapeDtypeStruct((length, part), BF),
+            jax.ShapeDtypeStruct((groups, 8, length), F32),
+        ),
+        in_specs=inputs,
+        out_specs=(rows, sums),
+        cost_estimate=pl.CostEstimate(
+            flops=4 * work, bytes_accessed=8 * length * part, transcendentals=work // head_dim
+        ),
+        name="attend",
+    )(prefix, qkv, qkv, qkv)
+
+
+def attend_back(qkv, prefix, back_attended, lse, head_dim):
+    length, part = back_attended.shape
+    groups = part // 128
+    inputs, rows, sums = attend_specs(length, groups)
+    work = length * length * part
+    return pl.pallas_call(
+        functools.partial(attend_back_kernel, head_dim),
+        grid=(groups,),
+        out_shape=jax.ShapeDtypeStruct((3, length, part), BF),
+        in_specs=inputs + [rows, sums],
+        out_specs=pl.BlockSpec((3, length, 128), lambda i: (0, 0, i)),
+        scratch_shapes=[pltpu.VMEM((length, head_dim), F32), pltpu.VMEM((length, head_dim), F32)],
+        cost_estimate=pl.CostEstimate(
+            flops=10 * work, bytes_accessed=14 * length * part, transcendentals=work // head_dim
+        ),
+        name="attend_back",
+    )(prefix, qkv, qkv, qkv, back_attended, lse)
 
 
 def body(
@@ -487,7 +488,6 @@
     own_rows, width = tokens.shape
     all_rows = 2 * own_rows
     head_dim = width // HEADS
-    heads_local = w_query.shape[1] // head_dim
     part = w_query.shape[1]
     rows = w_query.shape[0]
     experts, _, hidden = expert_in.shape
@@ -553,11 +553,9 @@
     normed_one, scale_one = norm_parts(tokens_all)
     first_rows = (normed_one * gain_one + bias_one).astype(BF)
     qkv = dot(first_rows, qkv_w).astype(BF)
-    queries, keys_all, values_all = qkv[:, :part], qkv[:, part : 2 * part], qkv[:, 2 * part :]
-    attended, logsums = attention_forward(
-        queries, keys_all, values_all, prefix, heads_local, head_dim, [(), in_lead, ()]
-    )
-    attended = after(attended, (in_crossed, out_lead))
+    attended, lse = attend(qkv, prefix, head_dim)
+    attended = after(attended, in_lead)
+
     attn_terms = dot_nt(attended, out_w).astype(BF)
     residual = tokens_all + (attn_terms.astype(F32) + swap(attn_terms).astype(F32))
     normed_two, scale_two = norm_parts(residual)
@@ -641,14 +639,12 @@
     in_near = ring.near(grads_in, in_via, BF)
     back_attended = dot(back_out, out_w).astype(BF)
     grad_out = dot_tn(back_out, attended).astype(BF)
-    back_qkv = attention_backward(
-        queries, keys_all, values_all, prefix, logsums, back_attended, heads_local, head_dim,
-        [(), (out_near, in_via), ()],
-    )
+    back_qkv = attend_back(qkv, prefix, back_attended, lse, head_dim)
     back_qkv = after(back_qkv, (in_near, grads_out))
     grads_in = ring.last(grads_in, in_near, BF)
-    grad_qkv = dot_tn(first_rows, back_qkv).astype(BF)
-    first_terms = dot_nt(back_qkv, qkv_w).astype(BF)
+    grad_qkv = jnp.concatenate([dot_tn(first_rows, back_qkv[i]).astype(BF) for i in range(3)], axis=1)
+    first_terms = sum(dot_nt(back_qkv[i], qkv_w[:, i * part : (i + 1) * part]) for i in range(3))
+    first_terms = first_terms.astype(BF)
     own_terms = lax.dynamic_slice_in_dim(first_terms, first_own, own_rows)
     other_terms = lax.dynamic_slice_in_dim(first_terms, own_rows - first_own, own_rows)
     back_first = own_terms.astype(F32) + swap(other_terms).astype(F32)

time: 494 us -> 424 us (0.86)
  matrix products: 134 us -> 70 us
  Pallas kernels: 75.6 us -> 114 us
  local copies, waits for them, and re-layouts: 61.6 us -> 27.2 us
  other arithmetic: 60.9 us -> 39.4 us
  waiting for transfers between devices: 117 us -> 127 us
    dot_general x21 -> x0, matrix products: 66.7 us -> none  [the longest x6 17.5 us: block_scores(): jnp.einsum('qhd,khd->hqk', query_rows, seq_keys, preferred_element_type=F32)]
    pallas_call x0 -> x2, Pallas kernels: none -> 39.4 us  [the longest x1 21.3 us: attend_back(): pl.pallas_call(functools.partial(attend_back_kernel, head_dim), grid=(gro...]
    slice x27 -> x1, local copies, waits for them, and re-layouts: 23.7 us -> 0.08 us  [far(): far[:half].astype(kind)]
    unnamed x210 -> x106, local copies, waits for them, and re-layouts: 17.6 us -> 6.81 us
    convert_element_type x2, other arithmetic: 12.6 us -> 2.54 us  [the longest x1 2.2 us: body(): first_rows = (normed_one * gain_one + bias_one).astype(BF)]
    ppermute x28, waiting for transfers between devices: 117 us -> 127 us  [move(): return lax.ppermute(value, 'dp', self.shift(stage, step))]
    concatenate x2 -> x3, other arithmetic: 8.93 us -> 1.52 us  [the longest x2 1.3 us: lead(): block = jnp.concatenate(parts, axis=0)]
    dot_general x8 -> x10, matrix products: 15.4 us -> 18.1 us  [dot_nt(): lax.dot_general(a, b, (((1,), (1,)), ((), ())), preferred_element_type=F32)]
  transfers between devices with their start and end apart: 35 -> 35, of which waited for: 14 -> 12; matrix products, arithmetic and copies ran while one was open for 47% -> 26% of each run, Pallas kernels for 0% -> 9%
where the time goes in v1:
time: 424 us; the launch traced here: 417 us
  waiting for transfers between devices  127 us (30%)
  Pallas kernels  114 us (27%)
  matrix products  70 us (17%)
  other arithmetic  39.4 us (9%)
  starting transfers between devices  36.4 us (9%)
  local copies, waits for them, and re-layouts  27.2 us (6%)
    ppermute x28, waiting for transfers between devices, move(): return lax.ppermute(value, 'dp', self.shift(stage, step))  127 us
    pallas_call x1, Pallas kernels, scatter_last(): pl.pallas_call(scatter_kernel, out_shape=(jax.ShapeDtypeStruct(small.shap...  40.2 us
    ppermute x28, starting transfers between devices, move(): return lax.ppermute(value, 'dp', self.shift(stage, step))  35.2 us
    pallas_call x1, Pallas kernels, gather_first(): pl.pallas_call(gather_kernel, out_shape=(jax.ShapeDtypeStruct((16, *vecto...  34.5 us
    dot_general x11, matrix products, dot(): lax.dot_general(a, b, (((1,), (0,)), ((), ())), preferred_element_type=F32)  32.8 us
    pallas_call x1, Pallas kernels, attend_back(): pl.pallas_call(functools.partial(attend_back_kernel, head_dim), grid=(gro...  21.3 us
    dot_general x10, matrix products, dot_tn(): lax.dot_general(a, b, (((0,), (0,)), ((), ())), preferred_element_type=F32)  19.1 us
    dot_general x10, matrix products, dot_nt(): lax.dot_general(a, b, (((1,), (1,)), ((), ())), preferred_element_type=F32)  18.1 us
  transfers between devices with their start and end apart: 35, of which 12 were waited for; matrix products, arithmetic and copies ran while one was open for 26% of the time, Pallas kernels for 9%

profile of v1, /device:TPU:0, one launch (start us, length us, event | category | flops | bytes accessed | tf_op | source)
XLA Modules:
  0.0 417.4 jit_solution(6215733016303698017)
XLA Ops:
  4.6 34.5 %gather_first.1 = (f32[16,8,128]{2,1,0:T(8,128)}, bf16[16,48,1536]{2,1,0:T(8,128)(2,1)}, f32[16,8,128]{2,1,0:T(8,128)}) custom-call(f32[8,128]{1,0:T(8,128)} %pad.8.vec_ref, bf16[48,1536]{1,0:T(8,128)(2,1)} %pad_maximum_fusion.9.qkv_ref), custom_call_target="tpu_custom_call" | custom-call | tf_op jit(solution)/shard_map/gather_first/pallas_call | solution.py:227
  52.9 4.3 %collective-permute-done.2 = bf16[48,3072]{1,0:T(8,128)(2,1)S(1)} collective-permute-done((bf16[48,3072]{1,0:T(8,128)(2,1)S(1)}, bf16[48,3072]{1,0:T(8,128)(2,1)S(1)}, u32[]{:S(2)}, u32[]{:S(2)}) %collective-permute-start.2) | collective-permute-done | bytes 294944 | tf_op jit(solution)/shard_map/ppermute | solution.py:56
  57.2 10.9 %collective-permute-done.1 = bf16[48,3072]{1,0:T(8,128)(2,1)S(1)} collective-permute-done((bf16[48,3072]{1,0:T(8,128)(2,1)S(1)}, bf16[48,3072]{1,0:T(8,128)(2,1)S(1)}, u32[]{:S(2)}, u32[]{:S(2)}) %collective-permute-start.1) | collective-permute-done | bytes 294944 | tf_op jit(solution)/shard_map/ppermute | solution.py:56
  80.7 3.7 convolution_convert_fusion.q_ref.k_ref.v_ref
  84.3 18.1 %attend.1 = (bf16[1024,384]{1,0:T(8,128)(2,1)}, f32[3,8,1024]{2,1,0:T(8,128)}) custom-call(s32[1]{0:T(128)S(6)} %copy.68.prefix_ref, bf16[1024,1152]{1,0:T(8,128)(2,1)} %convolution_convert_fusion.q_ref.k_ref.v_ref, bf16[1024,1152]{1,0:T(8,128)(2,1)} %convolution_convert_fusion.q_ref.k_ref.v_ref, bf16[1024,1152]{1,0:T(8,128)(2,1)} %convolution_convert_fusion.q_ref.k_ref.v_ref), custom_call_target="tpu_custom_call" | custom-call | flops 1610612736 | bytes 3145728 | tf_op jit(solution)/shard_map/attend/pallas_call | solution.py:434
  110.4 14.7 %collective-permute-done.8 = bf16[96,3072]{1,0:T(8,128)(2,1)S(1)} collective-permute-done((bf16[96,3072]{1,0:T(8,128)(2,1)S(1)}, bf16[96,3072]{1,0:T(8,128)(2,1)S(1)}, u32[]{:S(2)}, u32[]{:S(2)}) %collective-permute-start.8) | collective-permute-done | bytes 589856 | tf_op jit(solution)/shard_map/ppermute | solution.py:56
  134.2 4.2 %multiply_convert_fusion.1 = (bf16[640,1536]{1,0:T(8,128)(2,1)S(1)}, f32[640,1536]{1,0:T(8,128)}) fusion(bf16[768,3072]{1,0:T(8,128)(2,1)S(1)} %constant_dynamic-update-slice_fusion, bf16[1024,768]{1,0:T(8,128)(2,1)S(1)} %fusion.64), kind=kOutput, calls=%fused_computation.49 | convolution fusion | flops 1518796800 | bytes 9240576 | tf_op jit(solution)/shard_map/dot_general | solution.py:335
  151.5 9.9 %collective-permute-done.19 = bf16[96,3072]{1,0:T(8,128)(2,1)S(1)} collective-permute-done((bf16[96,3072]{1,0:T(8,128)(2,1)S(1)}, bf16[96,3072]{1,0:T(8,128)(2,1)S(1)}, u32[]{:S(2)}, u32[]{:S(2)}) %collective-permute-start.19) | collective-permute-done | bytes 589856 | tf_op jit(solution)/shard_map/ppermute | solution.py:56
  166.6 20.6 %collective-permute-done.14 = bf16[192,3072]{1,0:T(8,128)(2,1)S(1)} collective-permute-done((bf16[192,3072]{1,0:T(8,128)(2,1)S(1)}, bf16[192,3072]{1,0:T(8,128)(2,1)S(1)}, u32[]{:S(2)}, u32[]{:S(2)}) %collective-permute-start.14) | collective-permute-done | bytes 1179680 | tf_op jit(solution)/shard_map/ppermute | solution.py:56
  189.6 33.3 %collective-permute-done.15 = bf16[96,3072]{1,0:T(8,128)(2,1)S(1)} collective-permute-done((bf16[96,3072]{1,0:T(8,128)(2,1)S(1)}, bf16[96,3072]{1,0:T(8,128)(2,1)S(1)}, u32[]{:S(2)}, u32[]{:S(2)}) %collective-permute-start.15) | collective-permute-done | bytes 589856 | tf_op jit(solution)/shard_map/ppermute | solution.py:56
  226.8 4.1 fusion.10
  234.8 4.2 %fusion.17 = bf16[640,1536]{1,0:T(8,128)(2,1)S(1)} fusion(f32[640,1536]{1,0:T(8,128)S(1)} %get-tuple-element.115, bf16[640,768]{1,0:T(8,128)(2,1)S(1)} %slice_select_fusion, bf16[768,3072]{1,0:T(8,128)(2,1)S(1)} %constant_dynamic-update-slice_fusion.5), kind=kOutput, calls=%fused_computation.47 | convolution fusion | flops 1529610240 | bytes 9240576 | tf_op jit(solution)/shard_map/dot_general | solution.py:335
  243.7 3.3 fusion.70
  256.9 8.8 %collective-permute-done.23 = bf16[96,3072]{1,0:T(8,128)(2,1)S(1)} collective-permute-done((bf16[96,3072]{1,0:T(8,128)(2,1)S(1)}, bf16[96,3072]{1,0:T(8,128)(2,1)S(1)}, u32[]{:S(2)}, u32[]{:S(2)}) %collective-permute-start.23) | collective-permute-done | bytes 589856 | tf_op jit(solution)/shard_map/ppermute | solution.py:56
  272.2 10.6 %collective-permute-done.29 = bf16[48,3072]{1,0:T(8,128)(2,1)S(1)} collective-permute-done((bf16[48,3072]{1,0:T(8,128)(2,1)S(1)}, bf16[48,3072]{1,0:T(8,128)(2,1)S(1)}, u32[]{:S(2)}, u32[]{:S(2)}) %collective-permute-start.29) | collective-permute-done | bytes 294944 | tf_op jit(solution)/shard_map/ppermute | solution.py:56
  285.3 4.6 %fusion.25 = (f32[1024]{0:T(1024)S(1)}, f32[1024,768]{0,1:T(8,128)}) fusion(bf16[1024,768]{0,1:T(8,128)(2,1)S(1)} %fusion.63, bf16[1024,768]{0,1:T(8,128)(2,1)} %collective-permute-done.17, bf16[1024,768]{0,1:T(8,128)(2,1)} %fusion.70), kind=kLoop, calls=%fused_computation.63 | loop fusion | flops 4717568 | bytes 7868416 | tf_op jit(solution)/shard_map/reduce_sum | solution.py:623
  295.8 3.7 convert_add_fusion
  305.0 21.3 %attend_back.1 = bf16[3,1024,384]{2,1,0:T(8,128)(2,1)} custom-call(s32[1]{0:T(128)S(6)} %copy.68.prefix_ref, bf16[1024,1152]{1,0:T(8,128)(2,1)} %convolution_convert_fusion.q_ref.k_ref.v_ref, bf16[1024,1152]{1,0:T(8,128)(2,1)} %convolution_convert_fusion.q_ref.k_ref.v_ref, bf16[1024,1152]{1,0:T(8,128)(2,1)} %convolution_convert_fusion.q_ref.k_ref.v_ref, ...), custom_call_target="tpu_custom_call" | custom-call | flops 4026531840 | bytes 5505024 | tf_op jit(solution)/shard_map/attend_back/pallas_call | solution.py:455
  335.1 3.7 fusion.208
  339.6 3.4 collective-permute-start.32
  350.8 9.2 %collective-permute-done.34 = bf16[48,3072]{1,0:T(8,128)(2,1)} collective-permute-done((bf16[48,3072]{1,0:T(8,128)(2,1)S(1)}, bf16[48,3072]{1,0:T(8,128)(2,1)}, u32[]{:S(2)}, u32[]{:S(2)}) %collective-permute-start.34) | collective-permute-done | bytes 294944 | tf_op jit(solution)/shard_map/ppermute | solution.py:56
  360.0 3.8 collective-permute-done.33
  368.8 3.7 fusion.108
  373.4 40.2 %scatter_last.1 = (f32[8,128]{1,0:T(8,128)}, f32[48,1536]{1,0:T(8,128)}) custom-call(f32[16,8,128]{2,1,0:T(8,128)} %pad.9.small_ref, bf16[16,48,1536]{2,1,0:T(8,128)(2,1)} %bitcast.85), custom_call_target="tpu_custom_call" | custom-call | tf_op jit(solution)/shard_map/scatter_last/pallas_call | solution.py:311
  (284 shorter events, 135.2 us)
Async XLA Ops:
  43.0 25.1 %collective-permute-start.1 = (bf16[48,3072]{1,0:T(8,128)(2,1)S(1)}, bf16[48,3072]{1,0:T(8,128)(2,1)S(1)}, u32[]{:S(2)}, u32[]{:S(2)}) collective-permute-start(bf16[48,3072]{1,0:T(8,128)(2,1)S(1)} %bitcast.96), channel_id=1, source_target_pairs={{0,8},{2,10},{4,12},{6,14},{8,24},{10,26},{12,28},{14,30},{16,0},{... | collective-permute-start | bytes 884744 | tf_op jit(solution)/shard_map/ppermute | solution.py:56
  43.0 30.1 %collective-permute-start = (bf16[512,768]{1,0:T(8,128)(2,1)}, bf16[512,768]{1,0:T(8,128)(2,1)}, u32[]{:S(2)}, u32[]{:S(2)}) collective-permute-start(bf16[512,768]{1,0:T(8,128)(2,1)} %param.15), channel_id=1, source_target_pairs={{0,1},{1,0},{2,3},{3,2},{4,5},{5,4},{6,7},{7,6},{8,9},{9,8},{10,11... | collective-permute-start | bytes 2359304 | tf_op jit(solution)/shard_map/ppermute | solution.py:327
  43.0 61.9 %collective-permute-start.5 = (bf16[512,768]{1,0:T(8,128)(2,1)}, bf16[512,768]{1,0:T(8,128)(2,1)}, u32[]{:S(2)}, u32[]{:S(2)}) collective-permute-start(bf16[512,768]{1,0:T(8,128)(2,1)} %param.16), channel_id=1, source_target_pairs={{0,1},{1,0},{2,3},{3,2},{4,5},{5,4},{6,7},{7,6},{8,9},{9,8},{10,11... | collective-permute-start | bytes 2359304 | tf_op jit(solution)/shard_map/ppermute | solution.py:327
  68.2 78.0 %collective-permute-start.12 = (bf16[48,3072]{1,0:T(8,128)(2,1)}, bf16[48,3072]{1,0:T(8,128)(2,1)}, u32[]{:S(2)}, u32[]{:S(2)}) collective-permute-start(bf16[48,3072]{1,0:T(8,128)(2,1)} %bitcast.37), channel_id=1, source_target_pairs={{0,16},{2,18},{4,20},{6,22},{8,0},{10,2},{12,4},{14,6},{16,24},{18... | collective-permute-start | bytes 884744 | tf_op jit(solution)/shard_map/ppermute | solution.py:56
  68.3 78.0 %collective-permute-start.11 = (bf16[48,3072]{1,0:T(8,128)(2,1)}, bf16[48,3072]{1,0:T(8,128)(2,1)}, u32[]{:S(2)}, u32[]{:S(2)}) collective-permute-start(bf16[48,3072]{1,0:T(8,128)(2,1)} %bitcast.37), channel_id=1, source_target_pairs={{0,24},{2,26},{4,28},{6,30},{8,16},{10,18},{12,20},{14,22},{16,8},... | collective-permute-start | bytes 884744 | tf_op jit(solution)/shard_map/ppermute | solution.py:56
  70.5 37.4 %collective-permute-start.7 = (bf16[192,3072]{1,0:T(8,128)(2,1)S(1)}, bf16[192,3072]{1,0:T(8,128)(2,1)S(1)}, u32[]{:S(2)}, u32[]{:S(2)}) collective-permute-start(bf16[192,3072]{1,0:T(8,128)(2,1)S(1)} %pad_maximum_fusion.2), channel_id=1, source_target_pairs={{0,2},{2,0},{4,6},{6,4},{8,10},{10,8},{12,14},{14,12},{16,18},{18,... | collective-permute-start | bytes 3538952 | tf_op jit(solution)/shard_map/ppermute | solution.py:56
  73.1 36.5 %collective-permute-start.6 = (bf16[192,3072]{1,0:T(8,128)(2,1)S(1)}, bf16[192,3072]{1,0:T(8,128)(2,1)S(1)}, u32[]{:S(2)}, u32[]{:S(2)}) collective-permute-start(bf16[192,3072]{1,0:T(8,128)(2,1)S(1)} %pad_maximum_fusion.2), channel_id=1, source_target_pairs={{0,4},{2,6},{4,0},{6,2},{8,12},{10,14},{12,8},{14,10},{16,20},{18,... | collective-permute-start | bytes 3538952 | tf_op jit(solution)/shard_map/ppermute | solution.py:56
  104.9 21.3 %collective-permute-start.4 = (bf16[1024,768]{0,1:T(8,128)(2,1)S(1)}, bf16[1024,768]{0,1:T(8,128)(2,1)S(1)}, u32[]{:S(2)}, u32[]{:S(2)}) collective-permute-start(bf16[1024,768]{0,1:T(8,128)(2,1)S(1)} %convolution_convert_fusion.5), channel_id=1, source_target_pairs={{0,1},{1,0},{2,3},{3,2},{4,5},{5,4},{6,7},{7,6},{8,9},{9,8},{10,11... | collective-permute-start | bytes 4718600 | tf_op jit(solution)/shard_map/ppermute | solution.py:327
  108.0 18.2 %collective-permute-start.9 = (bf16[96,3072]{1,0:T(8,128)(2,1)S(1)}, bf16[96,3072]{1,0:T(8,128)(2,1)S(1)}, u32[]{:S(2)}, u32[]{:S(2)}) collective-permute-start(bf16[96,3072]{1,0:T(8,128)(2,1)S(1)} %slice.346), channel_id=1, source_target_pairs={{0,4},{2,6},{4,0},{6,2},{8,12},{10,14},{12,8},{14,10},{16,20},{18,... | collective-permute-start | bytes 1769480 | tf_op jit(solution)/shard_map/ppermute | solution.py:56
  125.1 21.1 %collective-permute-start.10 = (bf16[48,3072]{1,0:T(8,128)(2,1)}, bf16[48,3072]{1,0:T(8,128)(2,1)S(1)}, u32[]{:S(2)}, u32[]{:S(2)}) collective-permute-start(bf16[48,3072]{1,0:T(8,128)(2,1)} %bitcast.37), channel_id=1, source_target_pairs={{0,8},{2,10},{4,12},{6,14},{8,24},{10,26},{12,28},{14,30},{16,0},{... | collective-permute-start | bytes 884744 | tf_op jit(solution)/shard_map/ppermute | solution.py:56
  148.4 38.7 %collective-permute-start.14 = (bf16[192,3072]{1,0:T(8,128)(2,1)S(1)}, bf16[192,3072]{1,0:T(8,128)(2,1)S(1)}, u32[]{:S(2)}, u32[]{:S(2)}) collective-permute-start(bf16[192,3072]{1,0:T(8,128)(2,1)S(1)} %pad_maximum_fusion.3), channel_id=1, source_target_pairs={{0,2},{2,0},{4,6},{6,4},{8,10},{10,8},{12,14},{14,12},{16,18},{18,... | collective-permute-start | bytes 3538952 | tf_op jit(solution)/shard_map/ppermute | solution.py:56
  149.9 38.9 %collective-permute-start.13 = (bf16[192,3072]{1,0:T(8,128)(2,1)S(1)}, bf16[192,3072]{1,0:T(8,128)(2,1)S(1)}, u32[]{:S(2)}, u32[]{:S(2)}) collective-permute-start(bf16[192,3072]{1,0:T(8,128)(2,1)S(1)} %pad_maximum_fusion.3), channel_id=1, source_target_pairs={{0,4},{2,6},{4,0},{6,2},{8,12},{10,14},{12,8},{14,10},{16,20},{18,... | collective-permute-start | bytes 3538952 | tf_op jit(solution)/shard_map/ppermute | solution.py:56
  163.4 87.7 %collective-permute-start.26 = (bf16[192,3072]{1,0:T(8,128)(2,1)}, bf16[192,3072]{1,0:T(8,128)(2,1)}, u32[]{:S(2)}, u32[]{:S(2)}) collective-permute-start(bf16[192,3072]{1,0:T(8,128)(2,1)} %fusion.113), channel_id=1, source_target_pairs={{0,4},{2,6},{4,0},{6,2},{8,12},{10,14},{12,8},{14,10},{16,20},{18,... | collective-permute-start | bytes 3538952 | tf_op jit(solution)/shard_map/ppermute | solution.py:56
  166.1 86.7 %collective-permute-start.25 = (bf16[192,3072]{1,0:T(8,128)(2,1)}, bf16[192,3072]{1,0:T(8,128)(2,1)}, u32[]{:S(2)}, u32[]{:S(2)}) collective-permute-start(bf16[192,3072]{1,0:T(8,128)(2,1)} %pad_maximum_fusion.6), channel_id=1, source_target_pairs={{0,2},{2,0},{4,6},{6,4},{8,10},{10,8},{12,14},{14,12},{16,18},{18,... | collective-permute-start | bytes 3538952 | tf_op jit(solution)/shard_map/ppermute | solution.py:56
  187.2 35.7 %collective-permute-start.16 = (bf16[96,3072]{1,0:T(8,128)(2,1)S(1)}, bf16[96,3072]{1,0:T(8,128)(2,1)S(1)}, u32[]{:S(2)}, u32[]{:S(2)}) collective-permute-start(bf16[96,3072]{1,0:T(8,128)(2,1)S(1)} %slice.349), channel_id=1, source_target_pairs={{0,4},{2,6},{4,0},{6,2},{8,12},{10,14},{12,8},{14,10},{16,20},{18,... | collective-permute-start | bytes 1769480 | tf_op jit(solution)/shard_map/ppermute | solution.py:56
  188.9 34.0 %collective-permute-start.15 = (bf16[96,3072]{1,0:T(8,128)(2,1)S(1)}, bf16[96,3072]{1,0:T(8,128)(2,1)S(1)}, u32[]{:S(2)}, u32[]{:S(2)}) collective-permute-start(bf16[96,3072]{1,0:T(8,128)(2,1)S(1)} %slice.348), channel_id=1, source_target_pairs={{0,2},{2,0},{4,6},{6,4},{8,10},{10,8},{12,14},{14,12},{16,18},{18,... | collective-permute-start | bytes 1769480 | tf_op jit(solution)/shard_map/ppermute | solution.py:56
  247.0 38.4 %collective-permute-start.17 = (bf16[1024,768]{0,1:T(8,128)(2,1)}, bf16[1024,768]{0,1:T(8,128)(2,1)}, u32[]{:S(2)}, u32[]{:S(2)}) collective-permute-start(bf16[1024,768]{0,1:T(8,128)(2,1)} %fusion.70), channel_id=1, source_target_pairs={{0,1},{1,0},{2,3},{3,2},{4,5},{5,4},{6,7},{7,6},{8,9},{9,8},{10,11... | collective-permute-start | bytes 4718600 | tf_op jit(solution)/shard_map/ppermute | solution.py:327
  249.1 40.9 %collective-permute-start.20 = (bf16[1024,768]{0,1:T(8,128)(2,1)S(1)}, bf16[1024,768]{0,1:T(8,128)(2,1)S(1)}, u32[]{:S(2)}, u32[]{:S(2)}) collective-permute-start(bf16[1024,768]{0,1:T(8,128)(2,1)S(1)} %fusion.71), channel_id=1, source_target_pairs={{0,1},{1,0},{2,3},{3,2},{4,5},{5,4},{6,7},{7,6},{8,9},{9,8},{10,11... | collective-permute-start | bytes 4718600 | tf_op jit(solution)/shard_map/ppermute | solution.py:327
  265.7 17.1 %collective-permute-start.29 = (bf16[48,3072]{1,0:T(8,128)(2,1)S(1)}, bf16[48,3072]{1,0:T(8,128)(2,1)S(1)}, u32[]{:S(2)}, u32[]{:S(2)}) collective-permute-start(bf16[48,3072]{1,0:T(8,128)(2,1)S(1)} %get-tuple-element.98), channel_id=1, source_target_pairs={{0,8},{2,10},{4,12},{6,14},{8,24},{10,26},{12,28},{14,30},{16,0},{... | collective-permute-start | bytes 884744 | tf_op jit(solution)/shard_map/ppermute | solution.py:56
  266.7 17.7 %collective-permute-start.28 = (bf16[48,3072]{1,0:T(8,128)(2,1)S(1)}, bf16[48,3072]{1,0:T(8,128)(2,1)S(1)}, u32[]{:S(2)}, u32[]{:S(2)}) collective-permute-start(bf16[48,3072]{1,0:T(8,128)(2,1)S(1)} %get-tuple-element.99), channel_id=1, source_target_pairs={{0,24},{2,26},{4,28},{6,30},{8,16},{10,18},{12,20},{14,22},{16,8},... | collective-permute-start | bytes 884744 | tf_op jit(solution)/shard_map/ppermute | solution.py:56
  271.7 54.7 %collective-permute-start.22 = (bf16[192,3072]{1,0:T(8,128)(2,1)}, bf16[192,3072]{1,0:T(8,128)(2,1)}, u32[]{:S(2)}, u32[]{:S(2)}) collective-permute-start(bf16[192,3072]{1,0:T(8,128)(2,1)} %pad_maximum_fusion.4), channel_id=1, source_target_pairs={{0,2},{2,0},{4,6},{6,4},{8,10},{10,8},{12,14},{14,12},{16,18},{18,... | collective-permute-start | bytes 3538952 | tf_op jit(solution)/shard_map/ppermute | solution.py:56
  282.8 43.6 %collective-permute-start.24 = (bf16[192,3072]{1,0:T(8,128)(2,1)}, bf16[192,3072]{1,0:T(8,128)(2,1)}, u32[]{:S(2)}, u32[]{:S(2)}) collective-permute-start(bf16[192,3072]{1,0:T(8,128)(2,1)} %pad_maximum_fusion.5), channel_id=1, source_target_pairs={{0,4},{2,6},{4,0},{6,2},{8,12},{10,14},{12,8},{14,10},{16,20},{18,... | collective-permute-start | bytes 3538952 | tf_op jit(solution)/shard_map/ppermute | solution.py:56
  343.1 20.8 %collective-permute-start.33 = (bf16[48,3072]{1,0:T(8,128)(2,1)S(1)}, bf16[48,3072]{1,0:T(8,128)(2,1)}, u32[]{:S(2)}, u32[]{:S(2)}) collective-permute-start(bf16[48,3072]{1,0:T(8,128)(2,1)S(1)} %get-tuple-element.96), channel_id=1, source_target_pairs={{0,24},{2,26},{4,28},{6,30},{8,16},{10,18},{12,20},{14,22},{16,8},... | collective-permute-start | bytes 884744 | tf_op jit(solution)/shard_map/ppermute | solution.py:56
  347.9 18.3 %collective-permute-start.30 = (bf16[512,768]{0,1:T(8,128)(2,1)}, bf16[512,768]{0,1:T(8,128)(2,1)}, u32[]{:S(2)}, u32[]{:S(2)}) collective-permute-start(bf16[512,768]{0,1:T(8,128)(2,1)} %constant_dynamic-slice_fusion.1), channel_id=1, source_target_pairs={{0,1},{1,0},{2,3},{3,2},{4,5},{5,4},{6,7},{7,6},{8,9},{9,8},{10,11... | collective-permute-start | bytes 2359304 | tf_op jit(solution)/shard_map/ppermute | solution.py:327
  (62 other events, 735.7 us)

commit v2 on v1

--- a/solution.py
+++ b/solution.py
@@ -75,6 +75,12 @@
         from_x, from_y = crossed
         low, high = self.move(from_y[:half], x, 1), self.move(from_x[half:], y, 1)
         return jnp.concatenate([block, from_y, from_x, low, high], axis=0)
+
+    def along(self, blocks):
+        steps = [blocks] + [self.move(blocks, 0, step) for step in range(1, 4)]
+        rows, width = blocks.shape
+        joined = jnp.stack([step.reshape(4, rows // 4, width) for step in steps], axis=1)
+        return joined.reshape(4 * rows, width)
 
     def gather(self, block):
         block = self.lead(block)
@@ -149,178 +155,171 @@
     return along, me + 1 - 2 * (me % 2), me + 2 - 4 * ((me // 2) % 2)
 
 
-def greet(along, x_way, y_way, other):
+def greet(along, x_way, y_way):
     barrier = pltpu.get_barrier_semaphore()
     for device in along + [x_way, y_way]:
         pl.semaphore_signal(barrier, inc=1, device_id={"dp": device}, device_id_type=MESH)
-    pl.semaphore_signal(barrier, inc=1, device_id={"tensor": other}, device_id_type=MESH)
-    pl.semaphore_wait(barrier, 6)
-
-
-def gather_kernel(vec_ref, qkv_ref, vec_out, qkv_out, vec_other, send, recv, local):
+    pl.semaphore_wait(barrier, 5)
+
+
+CHUNK = 16
+
+
+def gather_kernel(block_ref, out_ref, send, recv, local):
     along, x_way, y_way = partners_of(lax.axis_index("dp"))
-    other = 1 - lax.axis_index("tensor")
-    greet(along, x_way, y_way, other)
-    blocks, outs = (vec_ref, qkv_ref), (vec_out, qkv_out)
+    greet(along, x_way, y_way)
+    chunks = block_ref.shape[0] // CHUNK
     copies = {}
 
-    def start(kind, source, slot, device):
+    def own(chunk):
+        return block_ref.at[pl.ds(chunk * CHUNK, CHUNK)]
+
+    def slot_of(chunk, slot):
+        return out_ref.at[slot, pl.ds(chunk * CHUNK, CHUNK)]
+
+    def start(chunk, source, slot, device):
         copy = pltpu.make_async_remote_copy(
             src_ref=source,
-            dst_ref=outs[kind].at[slot],
-            send_sem=send.at[kind, slot],
-            recv_sem=recv.at[kind, slot],
+            dst_ref=slot_of(chunk, slot),
+            send_sem=send.at[chunk, slot],
+            recv_sem=recv.at[chunk, slot],
             device_id={"dp": device},
             device_id_type=MESH,
         )
         copy.start()
-        copies[kind, slot] = copy
-
-    kept = []
-    for kind in range(2):
+        copies[chunk, slot] = copy
+
+    def pass_far(chunk):
+        for step in range(4):
+            slot = 4 + step if step < 2 else 8 + step
+            copies[chunk, slot].wait_recv()
+            start(chunk, slot_of(chunk, slot), 12 + step, x_way if step < 2 else y_way)
+
+    for chunk in range(chunks):
         for step in range(1, 4):
-            start(kind, blocks[kind], step, along[step - 1])
-        start(kind, blocks[kind], 4, y_way)
-        start(kind, blocks[kind], 8, x_way)
-        copy = pltpu.make_async_copy(blocks[kind], outs[kind].at[0], local.at[kind])
-        copy.start()
-        kept.append(copy)
-    for step in range(1, 4):
-        for kind in range(2):
-            copies[kind, step].wait_recv()
-            start(kind, outs[kind].at[step], 4 + step, y_way)
-            start(kind, outs[kind].at[step], 8 + step, x_way)
-        if step == 1:
-            for kind in range(2):
-                copies[kind, 4].wait_recv()
-                start(kind, outs[kind].at[4], 12, x_way)
-    for step in range(1, 4):
-        for kind in range(2):
-            slot = 4 + step if step < 2 else 8 + step
-            copies[kind, slot].wait_recv()
-            start(kind, outs[kind].at[slot], 12 + step, x_way if step < 2 else y_way)
-    waited = (1, 2, 3, 4, 5, 10, 11)
-    rest = [slot for slot in range(4, 16) if slot not in waited]
-    for slot in rest:
-        copies[0, slot].wait_recv()
-    kept[0].wait()
-    shared = pltpu.make_async_remote_copy(
-        src_ref=vec_out,
-        dst_ref=vec_other,
-        send_sem=send.at[0, 0],
-        recv_sem=recv.at[0, 0],
-        device_id={"tensor": other},
-        device_id_type=MESH,
-    )
-    shared.start()
-    for slot in rest:
-        copies[1, slot].wait_recv()
-    kept[1].wait()
+            start(chunk, own(chunk), step, along[step - 1])
+        start(chunk, own(chunk), 4, y_way)
+        start(chunk, own(chunk), 8, x_way)
+    kept = pltpu.make_async_copy(block_ref, out_ref.at[0], local)
+    kept.start()
+    for chunk in range(chunks):
+        for step in range(1, 4):
+            copies[chunk, step].wait_recv()
+            start(chunk, slot_of(chunk, step), 4 + step, y_way)
+            start(chunk, slot_of(chunk, step), 8 + step, x_way)
+        if chunk:
+            pass_far(chunk - 1)
+    pass_far(chunks - 1)
+    for chunk in range(chunks):
+        for slot in (6, 7, 8, 9, 12, 13, 14, 15):
+            copies[chunk, slot].wait_recv()
+    kept.wait()
     for copy in copies.values():
         copy.wait_send()
-    shared.wait()
-
-
-def gather_first(vectors, qkv):
-    anywhere = pl.BlockSpec(memory_space=pl.ANY)
-    inside = pl.BlockSpec(memory_space=pltpu.VMEM)
+
+
+def gather_first(block):
+    chunks = block.shape[0] // CHUNK
     return pl.pallas_call(
         gather_kernel,
-        out_shape=(
-            jax.ShapeDtypeStruct((16, *vectors.shape), vectors.dtype),
-            jax.ShapeDtypeStruct((16, *qkv.shape), qkv.dtype),
-            jax.ShapeDtypeStruct((16, *vectors.shape), vectors.dtype),
-        ),
-        in_specs=[inside, inside],
-        out_specs=(anywhere, anywhere, anywhere),
+        out_shape=jax.ShapeDtypeStruct((16, *block.shape), block.dtype),
+        in_specs=[pl.BlockSpec(memory_space=pltpu.VMEM)],
+        out_specs=pl.BlockSpec(memory_space=pl.ANY),
         scratch_shapes=[
-            pltpu.SemaphoreType.DMA((2, 16)),
-            pltpu.SemaphoreType.DMA((2, 16)),
-            pltpu.SemaphoreType.DMA((2,)),
+            pltpu.SemaphoreType.DMA((chunks, 16)),
+            pltpu.SemaphoreType.DMA((chunks, 16)),
+            pltpu.SemaphoreType.DMA,
         ],
         compiler_params=pltpu.CompilerParams(collective_id=0, has_side_effects=True),
         name="gather_first",
-    )(vectors, qkv)
-
-
-def scatter_kernel(
-    small_ref, grad_ref, small_out, grad_out,
-    small_via, small_fold, small_cross, small_sums, small_last,
-    grad_via, grad_fold, grad_cross, grad_sums, grad_last,
-    send, recv,
-):
+    )(block)
+
+
+def three_parts(values):
+    parts = []
+    for _ in range(3):
+        part = lax.reduce_precision(values, 8, 7)
+        parts.append(part.astype(BF))
+        values = values - part
+    return jnp.stack(parts)
+
+
+def scatter_kernel(blocks, out_ref, via, fold, cross, sums, last, send, recv):
     along, x_way, y_way = partners_of(lax.axis_index("dp"))
-    greet(along, x_way, y_way, 1 - lax.axis_index("tensor"))
-    blocks, results = (small_ref, grad_ref), (small_out, grad_out)
-    via, fold = (small_via, grad_via), (small_fold, grad_fold)
-    cross, sums, last = (small_cross, grad_cross), (small_sums, grad_sums), (small_last, grad_last)
+    greet(along, x_way, y_way)
+    chunks = out_ref.shape[0] // CHUNK
     copies = {}
 
-    def start(kind, source, target, number, device):
+    def at(buffer, chunk, slot):
+        return buffer.at[slot, pl.ds(chunk * CHUNK, CHUNK)]
+
+    def wide(buffer, chunk, slot):
+        return at(buffer, chunk, slot)[...].astype(F32)
+
+    def result(chunk):
+        return out_ref.at[pl.ds(chunk * CHUNK, CHUNK)]
+
+    def start(chunk, source, target, number, device):
         copy = pltpu.make_async_remote_copy(
             src_ref=source,
             dst_ref=target,
-            send_sem=send.at[kind, number],
-            recv_sem=recv.at[kind, number],
+            send_sem=send.at[chunk, number],
+            recv_sem=recv.at[chunk, number],
             device_id={"dp": device},
             device_id_type=MESH,
         )
         copy.start()
-        copies[kind, number] = copy
-
-    for kind in range(2):
+        copies[chunk, number] = copy
+
+    def close(chunk):
+        for step in (3, 1, 2, 0):
+            copies[chunk, 4 + step].wait_recv()
+            copies[chunk, 8 + step].wait_recv()
+            total = wide(blocks, chunk, step) + wide(cross, chunk, step) + wide(cross, chunk, 4 + step)
+            if step:
+                source = at(sums, chunk, step)
+                source[...] = total.astype(source.dtype)
+                start(chunk, source, at(last, chunk, step), 12 + step, along[3 - step])
+            else:
+                result(chunk)[...] = total
+
+    for chunk in range(chunks):
         for step in range(4):
             way = x_way if step < 2 else y_way
-            start(kind, blocks[kind].at[12 + step], via[kind].at[step], step, way)
-    for kind in range(2):
+            start(chunk, at(blocks, chunk, 12 + step), at(via, chunk, step), step, way)
         for step in range(2):
-            start(kind, blocks[kind].at[6 + step], cross[kind].at[2 + step], 6 + step, y_way)
-            start(kind, blocks[kind].at[8 + step], cross[kind].at[4 + step], 8 + step, x_way)
-    for step in (1, 3, 0, 2):
-        for kind in range(2):
+            start(chunk, at(blocks, chunk, 6 + step), at(cross, chunk, 2 + step), 6 + step, y_way)
+            start(chunk, at(blocks, chunk, 8 + step), at(cross, chunk, 4 + step), 8 + step, x_way)
+    for chunk in range(chunks):
+        for step in (1, 3, 0, 2):
             slot = 4 + step if step < 2 else 8 + step
-            copies[kind, step].wait_recv()
-            folded = blocks[kind][slot].astype(F32) + via[kind][step].astype(F32)
-            fold[kind][step] = folded.astype(fold[kind].dtype)
-            start(kind, fold[kind].at[step], cross[kind].at[slot - 4], slot, y_way if step < 2 else x_way)
-    for step in (3, 1, 2, 0):
-        for kind in range(2):
-            copies[kind, 4 + step].wait_recv()
-            copies[kind, 8 + step].wait_recv()
-            total = blocks[kind][step].astype(F32)
-            total = total + cross[kind][step].astype(F32) + cross[kind][4 + step].astype(F32)
-            if step:
-                sums[kind][step] = total.astype(sums[kind].dtype)
-                start(kind, sums[kind].at[step], last[kind].at[step], 12 + step, along[3 - step])
-            else:
-                results[kind][...] = total
-    for kind in range(2):
+            copies[chunk, step].wait_recv()
+            source = at(fold, chunk, step)
+            source[...] = (wide(blocks, chunk, slot) + wide(via, chunk, step)).astype(source.dtype)
+            start(chunk, source, at(cross, chunk, slot - 4), slot, y_way if step < 2 else x_way)
+        if chunk:
+            close(chunk - 1)
+    close(chunks - 1)
+    for chunk in range(chunks):
         for step in range(1, 4):
-            copies[kind, 12 + step].wait_recv()
-            results[kind][...] += last[kind][step].astype(F32)
+            copies[chunk, 12 + step].wait_recv()
+            result(chunk)[...] += wide(last, chunk, step)
     for copy in copies.values():
         copy.wait_send()
 
 
-def scatter_last(small, grads):
+def scatter_last(grads):
     inside = pl.BlockSpec(memory_space=pltpu.VMEM)
-    scratch = []
-    for value in (small, grads):
-        for slots in (4, 4, 8, 4, 4):
-            scratch.append(pltpu.VMEM((slots, *value.shape[1:]), value.dtype))
     return pl.pallas_call(
         scatter_kernel,
-        out_shape=(
-            jax.ShapeDtypeStruct(small.shape[1:], F32),
-            jax.ShapeDtypeStruct(grads.shape[1:], F32),
-        ),
-        in_specs=[inside, inside],
-        out_specs=(inside, inside),
-        scratch_shapes=scratch
-        + [pltpu.SemaphoreType.DMA((2, 16)), pltpu.SemaphoreType.DMA((2, 16))],
+        out_shape=jax.ShapeDtypeStruct(grads.shape[1:], F32),
+        in_specs=[inside],
+        out_specs=inside,
+        scratch_shapes=[pltpu.VMEM((slots, *grads.shape[1:]), grads.dtype) for slots in (4, 4, 8, 4, 4)]
+        + [pltpu.SemaphoreType.DMA((grads.shape[1] // CHUNK, 16))] * 2,
         compiler_params=pltpu.CompilerParams(collective_id=1, has_side_effects=True),
         name="scatter_last",
-    )(small, grads)
+    )(grads)
 
 
 def swap(value):
@@ -512,17 +511,23 @@
     small_count = vectors.shape[0]
     qkv_block = jnp.concatenate([w_query, w_key, w_value, w_out.T], axis=1)
     in_block = expert_in.transpose(1, 0, 2).reshape(rows, experts * hidden)
-    out_block = expert_out.transpose(2, 0, 1).reshape(rows, experts * hidden)
+    out_blocks = expert_out.transpose(2, 0, 1)
+    out_block, turned_block = out_blocks[:, 0], out_blocks[:, 1]
     if count == 16:
-        padded = jnp.pad(vectors, ((0, 8 - small_count), (0, 128 - rows // 2)))
-        table, qkv_w, other_table = gather_first(padded, qkv_block)
-        table, other_table = (t[:, :small_count, : rows // 2] for t in (table, other_table))
+        small_width = 3 * small_count * (rows // 2) // rows
+        extra = three_parts(vectors).reshape(rows, small_width)
+        extra = jnp.pad(extra, ((0, 0), (0, 128 - small_width)))
+        gathered = gather_first(jnp.concatenate([qkv_block, extra], axis=1))
+        parts = gathered[:, :, 4 * part : 4 * part + small_width].astype(F32)
+        parts = parts.reshape(count, 3, small_count, rows // 2)
+        table = (parts[:, 0] + parts[:, 1]) + parts[:, 2]
+        other_table = swap(table.reshape(count, -1)).reshape(table.shape)
         table = jnp.where(
             side == 0,
             jnp.concatenate([table, other_table], 2),
             jnp.concatenate([other_table, table], 2),
         )
-        qkv_w = qkv_w.reshape(width, 4 * part)
+        qkv_w = gathered.reshape(width, 4 * part + 128)
     else:
         other_vectors = swap(vectors)
         vectors = jnp.where(
@@ -536,14 +541,21 @@
     gain_one, bias_one, gain_two, bias_two = (table[i : i + 1] for i in range(4))
     centres = table[4:]
 
-    qkv_w, in_block = lax.optimization_barrier((qkv_w, in_block))
-    qkv_w, out_w = qkv_w[:, : 3 * part], qkv_w[:, 3 * part :]
+    qkv_w, in_block, turned_block = lax.optimization_barrier((qkv_w, in_block, turned_block))
+    qkv_w, out_w = qkv_w[:, : 3 * part], qkv_w[:, 3 * part : 4 * part]
     in_lead = ring.lead(in_block)
+    if count == 16:
+        turned_crossed = ring.cross(turned_block)
+        turned_square = ring.close(turned_block, turned_crossed)
+        in_lead, turned_square = lax.optimization_barrier((in_lead, turned_square))
+        turned_w = ring.along(turned_square)
+    else:
+        turned_w = ring.gather(turned_block)
     in_crossed = ring.cross(in_lead)
     out_lead = ring.lead(after(out_block, in_lead))
     in_w = ring.close(in_lead, in_crossed)
     out_crossed = ring.cross(after(out_lead, in_w))
-    back_w = ring.close(out_lead, out_crossed)
+    back_ws = (ring.close(out_lead, out_crossed), turned_w)
 
     found = ring.width_order(width)
     to_order = (jnp.arange(width, dtype=jnp.int32)[:, None] == found[None, :]).astype(BF)
@@ -595,8 +607,8 @@
     for e, (columns, rows_in, back_rows, up, activated) in enumerate(hidden_of):
         if e == 1:
             back_rows = after(back_rows, out_via)
-        slot_out.append(dot_nt(activated, back_w[:, columns]).astype(BF))
-        back_activated = dot(back_rows, back_w[:, columns])
+        slot_out.append(dot_nt(activated, back_ws[e]).astype(BF))
+        back_activated = dot(back_rows, back_ws[e])
         back_up = jax.vjp(jax.nn.gelu, up)[1](back_activated)[0].astype(BF)
         grads_in.append(dot_tn(rows_in, back_up).astype(BF))
         back_picked.append(dot_nt(back_up, in_w[:, columns]).astype(BF))
@@ -662,14 +674,15 @@
     small = jnp.concatenate(
         [one_part, grad_gain_two[None], grad_bias_two[None], grad_centre], axis=0
     )
-    small = small.reshape(small_count, count, rows).transpose(1, 0, 2)
-    grad_first = jnp.concatenate([grad_qkv, grad_out], axis=1)
     if count == 16:
-        small = jnp.pad(small, ((0, 0), (0, 8 - small_count), (0, 128 - rows)))
-        small, grad_first = scatter_last(small, grad_first.reshape(count, rows, 4 * part))
-        small = small[:small_count, :rows]
+        extra = jnp.pad(small.T.astype(BF), ((0, 0), (0, 128 - small_count)))
+        grad_first = jnp.concatenate([grad_qkv, grad_out, extra], axis=1)
+        grad_first = scatter_last(grad_first.reshape(count, rows, 4 * part + 128))
+        small = grad_first[:, 4 * part : 4 * part + small_count].T
+        grad_first = grad_first[:, : 4 * part]
     else:
-        grad_first = ring.scatter(grad_first, BF)
+        small = small.reshape(small_count, count, rows).transpose(1, 0, 2)
+        grad_first = ring.scatter(jnp.concatenate([grad_qkv, grad_out], axis=1), BF)
         small = ring.scatter(small.reshape(count, small_count * rows), F32).reshape(small_count, rows)
     grad_qkv, grad_out = grad_first[:, : 3 * part], grad_first[:, 3 * part :]
     small = lax.dynamic_slice_in_dim(small, side * (rows // 2), rows // 2, axis=1)

time: 424 us -> 441 us (1.040)
  local copies, waits for them, and re-layouts: 27.2 us -> 40.8 us
  other arithmetic: 39.4 us -> 28.7 us
  starting transfers between devices: 36.4 us -> 43.5 us
  waiting for transfers between devices: 127 us -> 132 us
    unnamed x106 -> x99, local copies, waits for them, and re-layouts: 6.81 us -> 19.9 us
    ppermute x28 -> x35, starting transfers between devices: 35.2 us -> 43.1 us  [move(): return lax.ppermute(value, 'dp', self.shift(stage, step))]
    ppermute x28 -> x35, waiting for transfers between devices: 127 us -> 132 us  [move(): return lax.ppermute(value, 'dp', self.shift(stage, step))]
  transfers between devices with their start and end apart: 35 -> 43, of which waited for: 12 -> 15; matrix products, arithmetic and copies ran while one was open for 26% -> 23% of each run, Pallas kernels for 9% -> 9%
where the time goes in v2:
time: 441 us; the launch traced here: 434 us
  waiting for transfers between devices  132 us (30%)
  Pallas kernels  116 us (26%)
  matrix products  68.6 us (16%)
  starting transfers between devices  43.5 us (10%)
  local copies, waits for them, and re-layouts  40.8 us (9%)
  other arithmetic  28.7 us (7%)
    ppermute x35, waiting for transfers between devices, move(): return lax.ppermute(value, 'dp', self.shift(stage, step))  132 us
    ppermute x35, starting transfers between devices, move(): return lax.ppermute(value, 'dp', self.shift(stage, step))  43.1 us
    pallas_call x1, Pallas kernels, scatter_last(): pl.pallas_call(scatter_kernel, out_shape=jax.ShapeDtypeStruct(grads.shape...  42.6 us
    pallas_call x1, Pallas kernels, gather_first(): pl.pallas_call(gather_kernel, out_shape=jax.ShapeDtypeStruct((16, *block....  34.8 us
    dot_general x11, matrix products, dot(): lax.dot_general(a, b, (((1,), (0,)), ((), ())), preferred_element_type=F32)  33 us
    pallas_call x1, Pallas kernels, attend_back(): pl.pallas_call(functools.partial(attend_back_kernel, head_dim), grid=(gro...  21.3 us
    unnamed x99, local copies, waits for them, and re-layouts  19.9 us
    dot_general x10, matrix products, dot_tn(): lax.dot_general(a, b, (((0,), (0,)), ((), ())), preferred_element_type=F32)  17.8 us
  transfers between devices with their start and end apart: 43, of which 15 were waited for; matrix products, arithmetic and copies ran while one was open for 23% of the time, Pallas kernels for 9%

profile of v2, /device:TPU:0, one launch (start us, length us, event | category | flops | bytes accessed | tf_op | source)
XLA Modules:
  0.0 433.8 jit_solution(11737331488219468778)
XLA Ops:
  7.3 34.8 %gather_first.1 = bf16[16,48,1664]{2,1,0:T(8,128)(2,1)} custom-call(bf16[48,1664]{1,0:T(8,128)(2,1)} %copy-done.21), custom_call_target="tpu_custom_call" | custom-call | tf_op jit(solution)/shard_map/gather_first/pallas_call | solution.py:223
  63.0 6.0 %collective-permute-done.2 = bf16[48,3072]{1,0:T(8,128)(2,1)S(1)} collective-permute-done((bf16[48,3072]{1,0:T(8,128)(2,1)S(1)}, bf16[48,3072]{1,0:T(8,128)(2,1)S(1)}, u32[]{:S(2)}, u32[]{:S(2)}) %collective-permute-start.2) | collective-permute-done | bytes 294944 | tf_op jit(solution)/shard_map/ppermute | solution.py:56
  74.5 4.2 collective-permute-done.17
  81.8 27.7 %collective-permute-done.15 = bf16[48,1536]{1,0:T(8,128)(2,1)S(1)} collective-permute-done((bf16[48,1536]{1,0:T(8,128)(2,1)S(1)}, bf16[48,1536]{1,0:T(8,128)(2,1)S(1)}, u32[]{:S(2)}, u32[]{:S(2)}) %collective-permute-start.15) | collective-permute-done | bytes 147488 | tf_op jit(solution)/shard_map/ppermute | solution.py:56
  116.8 3.7 convolution_convert_fusion.q_ref.k_ref.v_ref
  124.3 17.6 %attend.1 = (bf16[1024,384]{1,0:T(8,128)(2,1)}, f32[3,8,1024]{2,1,0:T(8,128)}) custom-call(s32[1]{0:T(128)S(6)} %copy.79.prefix_ref, bf16[1024,1152]{1,0:T(8,128)(2,1)} %convolution_convert_fusion.q_ref.k_ref.v_ref, bf16[1024,1152]{1,0:T(8,128)(2,1)} %convolution_convert_fusion.q_ref.k_ref.v_ref, bf16[1024,1152]{1,0:T(8,128)(2,1)} %convolution_convert_fusion.q_ref.k_ref.v_ref), custom_call_target="tpu_custom_call" | custom-call | flops 1610612736 | bytes 3145728 | tf_op jit(solution)/shard_map/attend/pallas_call | solution.py:433
  155.5 9.7 %collective-permute-done.13 = bf16[96,3072]{1,0:T(8,128)(2,1)S(1)} collective-permute-done((bf16[96,3072]{1,0:T(8,128)(2,1)S(1)}, bf16[96,3072]{1,0:T(8,128)(2,1)S(1)}, u32[]{:S(2)}, u32[]{:S(2)}) %collective-permute-start.13) | collective-permute-done | bytes 589856 | tf_op jit(solution)/shard_map/ppermute | solution.py:56
  176.7 4.2 multiply_convert_fusion.1
  193.9 16.6 %collective-permute-done.20 = bf16[96,1536]{1,0:T(8,128)(2,1)S(1)} collective-permute-done((bf16[96,1536]{1,0:T(8,128)(2,1)S(1)}, bf16[96,1536]{1,0:T(8,128)(2,1)S(1)}, u32[]{:S(2)}, u32[]{:S(2)}) %collective-permute-start.20) | collective-permute-done | bytes 294944 | tf_op jit(solution)/shard_map/ppermute | solution.py:56
  212.3 5.7 %fusion.10 = bf16[640,1536]{1,0:T(8,128)(2,1)S(1)} fusion(f32[640,1536]{1,0:T(8,128)} %get-tuple-element.142, bf16[768,1536]{1,0:T(8,128)(2,1)S(1)} %constant_dynamic-update-slice_fusion.15, bf16[1024,768]{1,0:T(8,128)(2,1)S(1)} %fusion.55, pred[640]{0:T(1024)(128)(4,1)S(1)} %get-tuple-element.95), kind=kOutput, calls=%fused_computation.40 | convolution fusion | flops 1530101760 | bytes 9241600 | tf_op jit(solution)/shard_map/dot_general | solution.py:334
  221.9 4.1 fusion.17
  234.6 3.2 fusion.58
  243.2 28.6 %collective-permute-done.31 = bf16[96,3072]{1,0:T(8,128)(2,1)S(1)} collective-permute-done((bf16[96,3072]{1,0:T(8,128)(2,1)S(1)}, bf16[96,3072]{1,0:T(8,128)(2,1)S(1)}, u32[]{:S(2)}, u32[]{:S(2)}) %collective-permute-start.31) | collective-permute-done | bytes 589856 | tf_op jit(solution)/shard_map/ppermute | solution.py:56
  281.5 5.5 %collective-permute-done.35 = bf16[48,3072]{1,0:T(8,128)(2,1)S(1)} collective-permute-done((bf16[48,3072]{1,0:T(8,128)(2,1)S(1)}, bf16[48,3072]{1,0:T(8,128)(2,1)S(1)}, u32[]{:S(2)}, u32[]{:S(2)}) %collective-permute-start.35) | collective-permute-done | bytes 294944 | tf_op jit(solution)/shard_map/ppermute | solution.py:56
  287.3 8.3 %collective-permute-done.37 = bf16[48,3072]{1,0:T(8,128)(2,1)S(1)} collective-permute-done((bf16[48,3072]{1,0:T(8,128)(2,1)S(1)}, bf16[48,3072]{1,0:T(8,128)(2,1)S(1)}, u32[]{:S(2)}, u32[]{:S(2)}) %collective-permute-start.37) | collective-permute-done | bytes 294944 | tf_op jit(solution)/shard_map/ppermute | solution.py:56
  296.1 5.4 %collective-permute-done.36 = bf16[48,3072]{1,0:T(8,128)(2,1)S(1)} collective-permute-done((bf16[48,3072]{1,0:T(8,128)(2,1)S(1)}, bf16[48,3072]{1,0:T(8,128)(2,1)S(1)}, u32[]{:S(2)}, u32[]{:S(2)}) %collective-permute-start.36) | collective-permute-done | bytes 294944 | tf_op jit(solution)/shard_map/ppermute | solution.py:56
  305.5 3.1 fusion.21
  316.5 3.0 convolution_convert_fusion.8.back_ref
  319.5 21.3 %attend_back.1 = bf16[3,1024,384]{2,1,0:T(8,128)(2,1)} custom-call(s32[1]{0:T(128)S(6)} %copy.79.prefix_ref, bf16[1024,1152]{1,0:T(8,128)(2,1)} %convolution_convert_fusion.q_ref.k_ref.v_ref, bf16[1024,1152]{1,0:T(8,128)(2,1)} %convolution_convert_fusion.q_ref.k_ref.v_ref, bf16[1024,1152]{1,0:T(8,128)(2,1)} %convolution_convert_fusion.q_ref.k_ref.v_ref, ...), custom_call_target="tpu_custom_call" | custom-call | flops 4026531840 | bytes 5505024 | tf_op jit(solution)/shard_map/attend_back/pallas_call | solution.py:454
  349.8 6.3 %collective-permute-start.40 = (bf16[48,3072]{1,0:T(8,128)(2,1)S(1)}, bf16[48,3072]{1,0:T(8,128)(2,1)S(1)}, u32[]{:S(2)}, u32[]{:S(2)}) collective-permute-start(bf16[48,3072]{1,0:T(8,128)(2,1)S(1)} %get-tuple-element.120), channel_id=1, source_target_pairs={{0,16},{2,18},{4,20},{6,22},{8,0},{10,2},{12,4},{14,6},{16,24},{18... | collective-permute-start | bytes 884744 | tf_op jit(solution)/shard_map/ppermute | solution.py:56
  363.6 9.4 %collective-permute-done.42 = bf16[48,3072]{1,0:T(8,128)(2,1)S(1)} collective-permute-done((bf16[48,3072]{1,0:T(8,128)(2,1)S(1)}, bf16[48,3072]{1,0:T(8,128)(2,1)S(1)}, u32[]{:S(2)}, u32[]{:S(2)}) %collective-permute-start.42) | collective-permute-done | bytes 294944 | tf_op jit(solution)/shard_map/ppermute | solution.py:56
  373.0 5.3 %collective-permute-done.41 = bf16[48,3072]{1,0:T(8,128)(2,1)S(1)} collective-permute-done((bf16[48,3072]{1,0:T(8,128)(2,1)S(1)}, bf16[48,3072]{1,0:T(8,128)(2,1)S(1)}, u32[]{:S(2)}, u32[]{:S(2)}) %collective-permute-start.41) | collective-permute-done | bytes 294944 | tf_op jit(solution)/shard_map/ppermute | solution.py:56
  382.9 4.1 copy.43
  387.0 42.6 %scatter_last.1 = f32[48,1664]{1,0:T(8,128)} custom-call(bf16[16,48,1664]{2,1,0:T(8,128)(2,1)} %bitcast.97), custom_call_target="tpu_custom_call" | custom-call | tf_op jit(solution)/shard_map/scatter_last/pallas_call | solution.py:313
  (305 shorter events, 149.7 us)
Async XLA Ops:
  43.2 19.8 %collective-permute-start.4 = (bf16[48,3072]{1,0:T(8,128)(2,1)S(1)}, bf16[48,3072]{1,0:T(8,128)(2,1)S(1)}, u32[]{:S(2)}, u32[]{:S(2)}) collective-permute-start(bf16[48,3072]{1,0:T(8,128)(2,1)S(1)} %bitcast.102), channel_id=1, source_target_pairs={{0,16},{2,18},{4,20},{6,22},{8,0},{10,2},{12,4},{14,6},{16,24},{18... | collective-permute-start | bytes 884744 | tf_op jit(solution)/shard_map/ppermute | solution.py:56
  52.6 59.1 %collective-permute-start = (bf16[512,768]{1,0:T(8,128)(2,1)S(1)}, bf16[512,768]{1,0:T(8,128)(2,1)S(1)}, u32[]{:S(2)}, u32[]{:S(2)}) collective-permute-start(bf16[512,768]{1,0:T(8,128)(2,1)S(1)} %copy-done.36), channel_id=1, source_target_pairs={{0,1},{1,0},{2,3},{3,2},{4,5},{5,4},{6,7},{7,6},{8,9},{9,8},{10,11... | collective-permute-start | bytes 2359304 | tf_op jit(solution)/shard_map/ppermute | solution.py:326
  62.4 58.1 %collective-permute-start.10 = (bf16[512,768]{1,0:T(8,128)(2,1)}, bf16[512,768]{1,0:T(8,128)(2,1)S(1)}, u32[]{:S(2)}, u32[]{:S(2)}) collective-permute-start(bf16[512,768]{1,0:T(8,128)(2,1)} %param.16), channel_id=1, source_target_pairs={{0,1},{1,0},{2,3},{3,2},{4,5},{5,4},{6,7},{7,6},{8,9},{9,8},{10,11... | collective-permute-start | bytes 2359304 | tf_op jit(solution)/shard_map/ppermute | solution.py:326
  71.0 38.6 %collective-permute-start.15 = (bf16[48,1536]{1,0:T(8,128)(2,1)S(1)}, bf16[48,1536]{1,0:T(8,128)(2,1)S(1)}, u32[]{:S(2)}, u32[]{:S(2)}) collective-permute-start(bf16[48,1536]{1,0:T(8,128)(2,1)S(1)} %get-tuple-element.37), channel_id=1, source_target_pairs={{0,8},{2,10},{4,12},{6,14},{8,24},{10,26},{12,28},{14,30},{16,0},{... | collective-permute-start | bytes 442376 | tf_op jit(solution)/shard_map/ppermute | solution.py:56
  78.6 65.6 %collective-permute-start.24 = (bf16[192,1536]{1,0:T(8,128)(2,1)}, bf16[192,1536]{1,0:T(8,128)(2,1)}, u32[]{:S(2)}, u32[]{:S(2)}) collective-permute-start(bf16[192,1536]{1,0:T(8,128)(2,1)} %constant_dynamic-update-slice_fusion.5), channel_id=1, source_target_pairs={{0,16},{2,18},{4,20},{6,22},{8,0},{10,2},{12,4},{14,6},{16,24},{18... | collective-permute-start | bytes 1769480 | tf_op jit(solution)/shard_map/ppermute | solution.py:56
  78.9 65.4 %collective-permute-start.23 = (bf16[192,1536]{1,0:T(8,128)(2,1)}, bf16[192,1536]{1,0:T(8,128)(2,1)}, u32[]{:S(2)}, u32[]{:S(2)}) collective-permute-start(bf16[192,1536]{1,0:T(8,128)(2,1)} %constant_dynamic-update-slice_fusion.5), channel_id=1, source_target_pairs={{0,24},{2,26},{4,28},{6,30},{8,16},{10,18},{12,20},{14,22},{16,8},... | collective-permute-start | bytes 1769480 | tf_op jit(solution)/shard_map/ppermute | solution.py:56
  109.5 36.7 %collective-permute-start.12 = (bf16[192,3072]{1,0:T(8,128)(2,1)}, bf16[192,3072]{1,0:T(8,128)(2,1)}, u32[]{:S(2)}, u32[]{:S(2)}) collective-permute-start(bf16[192,3072]{1,0:T(8,128)(2,1)} %pad_maximum_fusion.2), channel_id=1, source_target_pairs={{0,2},{2,0},{4,6},{6,4},{8,10},{10,8},{12,14},{14,12},{16,18},{18,... | collective-permute-start | bytes 3538952 | tf_op jit(solution)/shard_map/ppermute | solution.py:56
  111.8 36.8 %collective-permute-start.11 = (bf16[192,3072]{1,0:T(8,128)(2,1)}, bf16[192,3072]{1,0:T(8,128)(2,1)}, u32[]{:S(2)}, u32[]{:S(2)}) collective-permute-start(bf16[192,3072]{1,0:T(8,128)(2,1)} %pad_maximum_fusion.2), channel_id=1, source_target_pairs={{0,4},{2,6},{4,0},{6,2},{8,12},{10,14},{12,8},{14,10},{16,20},{18,... | collective-permute-start | bytes 3538952 | tf_op jit(solution)/shard_map/ppermute | solution.py:56
  120.5 23.8 %collective-permute-start.22 = (bf16[192,1536]{1,0:T(8,128)(2,1)}, bf16[192,1536]{1,0:T(8,128)(2,1)}, u32[]{:S(2)}, u32[]{:S(2)}) collective-permute-start(bf16[192,1536]{1,0:T(8,128)(2,1)} %constant_dynamic-update-slice_fusion.5), channel_id=1, source_target_pairs={{0,8},{2,10},{4,12},{6,14},{8,24},{10,26},{12,28},{14,30},{16,0},{... | collective-permute-start | bytes 1769480 | tf_op jit(solution)/shard_map/ppermute | solution.py:56
  144.2 24.8 %collective-permute-start.9 = (bf16[1024,768]{0,1:T(8,128)(2,1)S(1)}, bf16[1024,768]{0,1:T(8,128)(2,1)S(1)}, u32[]{:S(2)}, u32[]{:S(2)}) collective-permute-start(bf16[1024,768]{0,1:T(8,128)(2,1)S(1)} %convolution_convert_fusion.5), channel_id=1, source_target_pairs={{0,1},{1,0},{2,3},{3,2},{4,5},{5,4},{6,7},{7,6},{8,9},{9,8},{10,11... | collective-permute-start | bytes 4718600 | tf_op jit(solution)/shard_map/ppermute | solution.py:326
  167.0 24.7 %collective-permute-start.19 = (bf16[192,1536]{1,0:T(8,128)(2,1)S(1)}, bf16[192,1536]{1,0:T(8,128)(2,1)S(1)}, u32[]{:S(2)}, u32[]{:S(2)}) collective-permute-start(bf16[192,1536]{1,0:T(8,128)(2,1)S(1)} %copy-done.11), channel_id=1, source_target_pairs={{0,2},{2,0},{4,6},{6,4},{8,10},{10,8},{12,14},{14,12},{16,18},{18,... | collective-permute-start | bytes 1769480 | tf_op jit(solution)/shard_map/ppermute | solution.py:56
  167.8 24.8 %collective-permute-start.18 = (bf16[192,1536]{1,0:T(8,128)(2,1)S(1)}, bf16[192,1536]{1,0:T(8,128)(2,1)S(1)}, u32[]{:S(2)}, u32[]{:S(2)}) collective-permute-start(bf16[192,1536]{1,0:T(8,128)(2,1)S(1)} %copy-done.11), channel_id=1, source_target_pairs={{0,4},{2,6},{4,0},{6,2},{8,12},{10,14},{12,8},{14,10},{16,20},{18,... | collective-permute-start | bytes 1769480 | tf_op jit(solution)/shard_map/ppermute | solution.py:56
  189.6 32.3 %collective-permute-start.27 = (bf16[96,3072]{1,0:T(8,128)(2,1)S(1)}, bf16[96,3072]{1,0:T(8,128)(2,1)S(1)}, u32[]{:S(2)}, u32[]{:S(2)}) collective-permute-start(bf16[96,3072]{1,0:T(8,128)(2,1)S(1)} %get-tuple-element.108), channel_id=1, source_target_pairs={{0,4},{2,6},{4,0},{6,2},{8,12},{10,14},{12,8},{14,10},{16,20},{18,... | collective-permute-start | bytes 1769480 | tf_op jit(solution)/shard_map/ppermute | solution.py:56
  190.5 31.4 %collective-permute-start.26 = (bf16[96,3072]{1,0:T(8,128)(2,1)S(1)}, bf16[96,3072]{1,0:T(8,128)(2,1)S(1)}, u32[]{:S(2)}, u32[]{:S(2)}) collective-permute-start(bf16[96,3072]{1,0:T(8,128)(2,1)S(1)} %get-tuple-element.109), channel_id=1, source_target_pairs={{0,2},{2,0},{4,6},{6,4},{8,10},{10,8},{12,14},{14,12},{16,18},{18,... | collective-permute-start | bytes 1769480 | tf_op jit(solution)/shard_map/ppermute | solution.py:56
  231.3 42.0 %collective-permute-start.34 = (bf16[192,3072]{1,0:T(8,128)(2,1)S(1)}, bf16[192,3072]{1,0:T(8,128)(2,1)}, u32[]{:S(2)}, u32[]{:S(2)}) collective-permute-start(bf16[192,3072]{1,0:T(8,128)(2,1)S(1)} %fusion.99), channel_id=1, source_target_pairs={{0,4},{2,6},{4,0},{6,2},{8,12},{10,14},{12,8},{14,10},{16,20},{18,... | collective-permute-start | bytes 3538952 | tf_op jit(solution)/shard_map/ppermute | solution.py:56
  233.7 39.6 %collective-permute-start.33 = (bf16[192,3072]{1,0:T(8,128)(2,1)}, bf16[192,3072]{1,0:T(8,128)(2,1)}, u32[]{:S(2)}, u32[]{:S(2)}) collective-permute-start(bf16[192,3072]{1,0:T(8,128)(2,1)} %pad_maximum_fusion.5), channel_id=1, source_target_pairs={{0,2},{2,0},{4,6},{6,4},{8,10},{10,8},{12,14},{14,12},{16,18},{18,... | collective-permute-start | bytes 3538952 | tf_op jit(solution)/shard_map/ppermute | solution.py:56
  237.8 64.8 %collective-permute-start.25 = (bf16[1024,768]{0,1:T(8,128)(2,1)}, bf16[1024,768]{0,1:T(8,128)(2,1)}, u32[]{:S(2)}, u32[]{:S(2)}) collective-permute-start(bf16[1024,768]{0,1:T(8,128)(2,1)} %fusion.58), channel_id=1, source_target_pairs={{0,1},{1,0},{2,3},{3,2},{4,5},{5,4},{6,7},{7,6},{8,9},{9,8},{10,11... | collective-permute-start | bytes 4718600 | tf_op jit(solution)/shard_map/ppermute | solution.py:326
  238.5 33.3 %collective-permute-start.31 = (bf16[96,3072]{1,0:T(8,128)(2,1)S(1)}, bf16[96,3072]{1,0:T(8,128)(2,1)S(1)}, u32[]{:S(2)}, u32[]{:S(2)}) collective-permute-start(bf16[96,3072]{1,0:T(8,128)(2,1)S(1)} %get-tuple-element.114), channel_id=1, source_target_pairs={{0,2},{2,0},{4,6},{6,4},{8,10},{10,8},{12,14},{14,12},{16,18},{18,... | collective-permute-start | bytes 1769480 | tf_op jit(solution)/shard_map/ppermute | solution.py:56
  239.8 32.0 %collective-permute-start.29 = (bf16[96,3072]{1,0:T(8,128)(2,1)S(1)}, bf16[96,3072]{1,0:T(8,128)(2,1)S(1)}, u32[]{:S(2)}, u32[]{:S(2)}) collective-permute-start(bf16[96,3072]{1,0:T(8,128)(2,1)S(1)} %get-tuple-element.115), channel_id=1, source_target_pairs={{0,4},{2,6},{4,0},{6,2},{8,12},{10,14},{12,8},{14,10},{16,20},{18,... | collective-permute-start | bytes 1769480 | tf_op jit(solution)/shard_map/ppermute | solution.py:56
  271.8 33.7 %collective-permute-start.28 = (bf16[1024,768]{0,1:T(8,128)(2,1)S(1)}, bf16[1024,768]{0,1:T(8,128)(2,1)S(1)}, u32[]{:S(2)}, u32[]{:S(2)}) collective-permute-start(bf16[1024,768]{0,1:T(8,128)(2,1)S(1)} %fusion.59), channel_id=1, source_target_pairs={{0,1},{1,0},{2,3},{3,2},{4,5},{5,4},{6,7},{7,6},{8,9},{9,8},{10,11... | collective-permute-start | bytes 4718600 | tf_op jit(solution)/shard_map/ppermute | solution.py:326
  279.1 22.5 %collective-permute-start.36 = (bf16[48,3072]{1,0:T(8,128)(2,1)S(1)}, bf16[48,3072]{1,0:T(8,128)(2,1)S(1)}, u32[]{:S(2)}, u32[]{:S(2)}) collective-permute-start(bf16[48,3072]{1,0:T(8,128)(2,1)S(1)} %get-tuple-element.125), channel_id=1, source_target_pairs={{0,24},{2,26},{4,28},{6,30},{8,16},{10,18},{12,20},{14,22},{16,8},... | collective-permute-start | bytes 884744 | tf_op jit(solution)/shard_map/ppermute | solution.py:56
  287.0 53.8 %collective-permute-start.30 = (bf16[192,3072]{1,0:T(8,128)(2,1)S(1)}, bf16[192,3072]{1,0:T(8,128)(2,1)}, u32[]{:S(2)}, u32[]{:S(2)}) collective-permute-start(bf16[192,3072]{1,0:T(8,128)(2,1)S(1)} %pad_maximum_fusion.3), channel_id=1, source_target_pairs={{0,2},{2,0},{4,6},{6,4},{8,10},{10,8},{12,14},{14,12},{16,18},{18,... | collective-permute-start | bytes 3538952 | tf_op jit(solution)/shard_map/ppermute | solution.py:56
  295.7 45.1 %collective-permute-start.32 = (bf16[192,3072]{1,0:T(8,128)(2,1)}, bf16[192,3072]{1,0:T(8,128)(2,1)}, u32[]{:S(2)}, u32[]{:S(2)}) collective-permute-start(bf16[192,3072]{1,0:T(8,128)(2,1)} %pad_maximum_fusion.4), channel_id=1, source_target_pairs={{0,4},{2,6},{4,0},{6,2},{8,12},{10,14},{12,8},{14,10},{16,20},{18,... | collective-permute-start | bytes 3538952 | tf_op jit(solution)/shard_map/ppermute | solution.py:56
  356.5 21.9 %collective-permute-start.41 = (bf16[48,3072]{1,0:T(8,128)(2,1)S(1)}, bf16[48,3072]{1,0:T(8,128)(2,1)S(1)}, u32[]{:S(2)}, u32[]{:S(2)}) collective-permute-start(bf16[48,3072]{1,0:T(8,128)(2,1)S(1)} %get-tuple-element.122), channel_id=1, source_target_pairs={{0,24},{2,26},{4,28},{6,30},{8,16},{10,18},{12,20},{14,22},{16,8},... | collective-permute-start | bytes 884744 | tf_op jit(solution)/shard_map/ppermute | solution.py:56
  (64 other events, 901.2 us)
